TPU v7x, 512 devices: a whole 4x4x16 slice. The times are simulated.
512 devices in a mesh: row: 16 (over x, y), col: 32 (over z, core).
Axes of the slice: x: 4, y: 4, z: 16, core: 2. Of those that a mesh axis runs over, the one named last changes fastest.
Arguments:
- arrival: float32 [64, 16384], P(None, 'col'), may hold values from 0 to 4
- delay: bfloat16 [4, 16384, 16384], P(None, 'col', 'row'), may hold values from -40 to 20
- occupancy: int32 [4, 32, 32], replicated, may hold values from 0 to 1, as said below
Outputs:
- final_arrival: float32 [64, 16384], P(None, 'col')
- worst: float32 [64], replicated
Inputs may be any that keep to these rules, and one draw needn't show every extreme that they name: In every level every column of tiles holds at least one tile with occupancy 1.
All inputs are finite; a program needn't handle non-finite values.
Results may differ from a plain program's by a relative error of at most 0.0009.
Values sent between devices are 32-bit elements; how exact they have to be, the bound alone decides.
No kernel may reach another device: no remote copies, remote signals or barrier semaphores. Data moves between devices by JAX's collectives and lax.ppermute only.
A program may use at most 64 MiB of HBM per device.

v0:
```python
import jax
import jax.numpy as jnp
from jax import lax
from jax.sharding import PartitionSpec as P


def from_everyone(shard, axis):
    copies = jnp.broadcast_to(shard, (lax.axis_size(axis), *shard.shape))
    return lax.all_to_all(copies, axis, split_axis=0, concat_axis=0, tiled=True)


def laid_out(tiles, dim):
    lengths = list(tiles.shape[1:])
    lengths[dim] *= tiles.shape[0]
    return jnp.moveaxis(tiles, 0, dim).reshape(lengths)


def gathered_copies(shard, axis, dim):
    tiles = from_everyone(shard, axis)
    return laid_out(tiles, dim)


def taken_together(shard, axis):
    return from_everyone(shard, axis).max(axis=0)


def level_max(times, delay_tile, keep):
    masked = jnp.where(keep[None, :], delay_tile.astype(jnp.float32), jnp.float32(-1000000000.0))
    rows = masked.shape[0]
    width = min(32, rows)
    turns = rows // width
    init = jnp.full((times.shape[0], masked.shape[1]), -1000000000.0, jnp.float32)

    def step(index, best):
        start = index * width
        part_a = lax.dynamic_slice_in_dim(times, start, width, 1)
        part_d = lax.dynamic_slice_in_dim(masked, start, width, 0)
        return jnp.maximum(best, jnp.max(part_a[:, :, None] + part_d[None, :, :], axis=1))

    return lax.fori_loop(0, turns, step, init)


def reduce_pieces(pieces):
    return jnp.max(pieces, axis=1)


def shards(arrival, delay, occupancy):
    col_count = lax.axis_size("col")
    row_count = lax.axis_size("row")
    ratio = col_count // row_count
    tile = arrival.shape[1]
    scenarios = arrival.shape[0]
    col_place = lax.axis_index("col")
    row_place = lax.axis_index("row")
    slice_pins = tile // row_count
    times = arrival
    for level in range(delay.shape[0]):
        flags = lax.dynamic_slice(occupancy[level], (col_place, row_place * ratio), (1, ratio))[0]
        keep = jnp.repeat(flags > 0, tile)
        partial_value = level_max(times, delay[level], keep)
        shaped = partial_value.reshape(scenarios, col_count, slice_pins)
        reduced = reduce_pieces(
            lax.all_to_all(shaped, "col", split_axis=1, concat_axis=1, tiled=True)
        )
        gathered = gathered_copies(reduced[None], "row", 0)
        outgoing = jnp.repeat(gathered, ratio, axis=0)
        arrived = lax.all_to_all(outgoing, "col", split_axis=0, concat_axis=0, tiled=True)
        start = col_place % ratio * row_count
        mine = lax.dynamic_slice_in_dim(arrived, start, row_count, 0)
        times = jnp.transpose(mine, (1, 0, 2)).reshape(scenarios, tile)
    worst = taken_together(jnp.max(times, axis=1), "col")
    return (times, worst)


def solution(mesh):
    placed = (P(None, "col"), P(None, "col", "row"), P())
    return jax.shard_map(
        shards, mesh=mesh, in_specs=placed, out_specs=(P(None, "col"), P()), check_vma=False
    )
```

profile of v0, /device:TPU:1, one launch (start us, length us, event | category | flops | bytes accessed | tf_op | source)
XLA Modules:
  0.0 488.1 jit_solution(14964154743765826624)
XLA Ops:
  2.0 5.4 %convert_select_fusion = (f32[512,1024]{1,0:T(8,128)S(1)}, f32[512,1024]{1,0:T(8,128)}, f32[512,1024]{1,0:T(8,128)}, f32[512,1024]{1,0:T(8,128)}) fusion(bf16[4,512,1024]{2,1,0:T(8,128)(2,1)} %param.12, pred[1024]{0:T(1024)(128)(4,1)S(1)} %broadcast_in_dim.122, pred[1024]{0:T(1024)(128)(4,1)S(1)} %broadcast_in_dim.112, ...), kind=kLoop, calls=%fused_computation.16 | loop fusion | flops 4194304 | bytes 12587008 | tf_op jit(solution)/shard_map/jit(_where)/select_n | solution.py:28
  7.4 55.0 %while.56 = (s32[]{:T(128)}, f32[64,1024]{1,0:T(8,128)S(1)}, f32[64,512]{1,0:T(8,128)}, f32[512,1024]{1,0:T(8,128)}, s32[]{:T(128)}, /*index=5*/s32[]{:T(128)}, s32[]{:T(128)}, s32[]{:T(128)}) while((s32[]{:T(128)}, f32[64,1024]{1,0:T(8,128)S(1)}, f32[64,512]{1,0:T(8,128)}, f32[512,1024]{1,0:T(8,128)}, s32[]{:T(128)}, ...), condition=%wide.region_2.3_spmd.clone, body=%wide.region_0.2_spmd.clone.sunk | while | flops 4259847 | bytes 1466517 | solution.py:40
  9.1 1.6 add_reduce_fusion.8
  12.5 1.6 add_reduce_fusion.8
  62.9 38.8 %all_to_all.66 = f32[32,1,2048]{2,1,0:T(1,128)S(1)} all-to-all(f32[32,1,2048]{2,1,0:T(1,128)S(1)} %reshape.112), channel_id=1, replica_groups=mesh['row'=16,'col'=32] {'col'}, dimensions={0} | all-to-all | bytes 524288 | tf_op jit(solution)/shard_map/all_to_all | solution.py:63
  104.0 13.4 %all_to_all.67 = f32[16,1,2048]{2,1,0:T(1,128)S(1)} all-to-all(f32[16,1,2048]{2,1,0:T(1,128)S(1)} %reshape.114), channel_id=1, replica_groups=mesh['row'=16,'col'=32] {'row'}, dimensions={0} | all-to-all | bytes 262144 | tf_op jit(solution)/shard_map/all_to_all | solution.py:9
  119.5 5.5 %all-to-all-start.2 = ((f32[32,1,2048]{2,1,0:T(1,128)}), f32[32,1,2048]{2,1,0:T(1,128)S(1)}, u32[]{:S(2)}, u32[]{:S(2)}) async-start(f32[32,1,2048]{2,1,0:T(1,128)} %reshape.116), calls=%async_computation.2 | async-start | bytes 524288 | tf_op jit(solution)/shard_map/all_to_all | solution.py:67
  125.0 21.6 %all-to-all-done.2 = f32[32,1,2048]{2,1,0:T(1,128)S(1)} async-done(((f32[32,1,2048]{2,1,0:T(1,128)}), f32[32,1,2048]{2,1,0:T(1,128)S(1)}, u32[]{:S(2)}, u32[]{:S(2)}) %all-to-all-start.2) | async-done | bytes 262176 | tf_op jit(solution)/shard_map/all_to_all | solution.py:67
  148.1 42.9 %while.57 = (s32[]{:T(128)}, f32[64,1024]{1,0:T(8,128)S(1)}, f32[64,512]{0,1:T(8,128)S(1)}, f32[512,1024]{1,0:T(8,128)}, s32[]{:T(128)}, /*index=5*/s32[]{:T(128)}, s32[]{:T(128)}, s32[]{:T(128)}) while((s32[]{:T(128)}, f32[64,1024]{1,0:T(8,128)S(1)}, f32[64,512]{0,1:T(8,128)S(1)}, f32[512,1024]{1,0:T(8,128)}, s32[]{:T(128)}, ...), condition=%wide.region_6.7_spmd.clone, body=%wide.region_4.6_spmd.clone.sunk | while | flops 4259847 | bytes 1482901 | solution.py:40
  191.6 25.8 %all_to_all.68 = f32[32,1,2048]{2,1,0:T(1,128)S(1)} all-to-all(f32[32,1,2048]{2,1,0:T(1,128)S(1)} %reshape.118), channel_id=1, replica_groups=mesh['row'=16,'col'=32] {'col'}, dimensions={0} | all-to-all | bytes 524288 | tf_op jit(solution)/shard_map/all_to_all | solution.py:63
  219.1 9.9 %all_to_all.69 = f32[16,1,2048]{2,1,0:T(1,128)S(1)} all-to-all(f32[16,1,2048]{2,1,0:T(1,128)S(1)} %reshape.120), channel_id=1, replica_groups=mesh['row'=16,'col'=32] {'row'}, dimensions={0} | all-to-all | bytes 262144 | tf_op jit(solution)/shard_map/all_to_all | solution.py:9
  231.2 6.5 %all-to-all-start.5 = ((f32[32,1,2048]{2,1,0:T(1,128)}), f32[32,1,2048]{2,1,0:T(1,128)S(1)}, u32[]{:S(2)}, u32[]{:S(2)}) async-start(f32[32,1,2048]{2,1,0:T(1,128)} %reshape.122), calls=%async_computation.5 | async-start | bytes 524288 | tf_op jit(solution)/shard_map/all_to_all | solution.py:67
  237.7 21.6 %all-to-all-done.5 = f32[32,1,2048]{2,1,0:T(1,128)S(1)} async-done(((f32[32,1,2048]{2,1,0:T(1,128)}), f32[32,1,2048]{2,1,0:T(1,128)S(1)}, u32[]{:S(2)}, u32[]{:S(2)}) %all-to-all-start.5) | async-done | bytes 262176 | tf_op jit(solution)/shard_map/all_to_all | solution.py:67
  260.9 42.9 %while.58 = (s32[]{:T(128)}, f32[64,1024]{1,0:T(8,128)S(1)}, f32[64,512]{0,1:T(8,128)S(1)}, f32[512,1024]{1,0:T(8,128)}, s32[]{:T(128)}, /*index=5*/s32[]{:T(128)}, s32[]{:T(128)}, s32[]{:T(128)}) while((s32[]{:T(128)}, f32[64,1024]{1,0:T(8,128)S(1)}, f32[64,512]{0,1:T(8,128)S(1)}, f32[512,1024]{1,0:T(8,128)}, s32[]{:T(128)}, ...), condition=%wide.region_10.11_spmd.clone, body=%wide.region_8.10_spmd.clone.sunk | while | flops 4259847 | bytes 1482901 | solution.py:40
  304.3 25.8 %all_to_all.70 = f32[32,1,2048]{2,1,0:T(1,128)S(1)} all-to-all(f32[32,1,2048]{2,1,0:T(1,128)S(1)} %reshape.124), channel_id=1, replica_groups=mesh['row'=16,'col'=32] {'col'}, dimensions={0} | all-to-all | bytes 524288 | tf_op jit(solution)/shard_map/all_to_all | solution.py:63
  331.8 9.9 %all_to_all.71 = f32[16,1,2048]{2,1,0:T(1,128)S(1)} all-to-all(f32[16,1,2048]{2,1,0:T(1,128)S(1)} %reshape.126), channel_id=1, replica_groups=mesh['row'=16,'col'=32] {'row'}, dimensions={0} | all-to-all | bytes 262144 | tf_op jit(solution)/shard_map/all_to_all | solution.py:9
  343.9 6.4 %all-to-all-start.8 = ((f32[32,1,2048]{2,1,0:T(1,128)}), f32[32,1,2048]{2,1,0:T(1,128)S(1)}, u32[]{:S(2)}, u32[]{:S(2)}) async-start(f32[32,1,2048]{2,1,0:T(1,128)} %reshape.128), calls=%async_computation.8 | async-start | bytes 524288 | tf_op jit(solution)/shard_map/all_to_all | solution.py:67
  350.3 21.6 %all-to-all-done.8 = f32[32,1,2048]{2,1,0:T(1,128)S(1)} async-done(((f32[32,1,2048]{2,1,0:T(1,128)}), f32[32,1,2048]{2,1,0:T(1,128)S(1)}, u32[]{:S(2)}, u32[]{:S(2)}) %all-to-all-start.8) | async-done | bytes 262176 | tf_op jit(solution)/shard_map/all_to_all | solution.py:67
  373.4 28.5 %while.59 = (s32[]{:T(128)}, f32[64,1024]{1,0:T(8,128)S(1)}, f32[64,512]{0,1:T(8,128)S(1)}, f32[512,1024]{1,0:T(8,128)S(1)}, s32[]{:T(128)}, /*index=5*/s32[]{:T(128)}, s32[]{:T(128)}, s32[]{:T(128)}) while((s32[]{:T(128)}, f32[64,1024]{1,0:T(8,128)S(1)}, f32[64,512]{0,1:T(8,128)S(1)}, f32[512,1024]{1,0:T(8,128)S(1)}, ...), condition=%wide.region_14.15_spmd.clone, body=%wide.region_12.14_spmd.clone.sunk | while | flops 4259847 | bytes 1482901 | solution.py:40
  402.5 25.8 %all_to_all.72 = f32[32,1,2048]{2,1,0:T(1,128)S(1)} all-to-all(f32[32,1,2048]{2,1,0:T(1,128)S(1)} %reshape.130), channel_id=1, replica_groups=mesh['row'=16,'col'=32] {'col'}, dimensions={0} | all-to-all | bytes 524288 | tf_op jit(solution)/shard_map/all_to_all | solution.py:63
  430.0 9.9 %all_to_all.73 = f32[16,1,2048]{2,1,0:T(1,128)S(1)} all-to-all(f32[16,1,2048]{2,1,0:T(1,128)S(1)} %reshape.132), channel_id=1, replica_groups=mesh['row'=16,'col'=32] {'row'}, dimensions={0} | all-to-all | bytes 262144 | tf_op jit(solution)/shard_map/all_to_all | solution.py:9
  441.4 27.1 %all_to_all.74 = f32[32,1,2048]{2,1,0:T(1,128)S(1)} all-to-all(f32[32,1,2048]{2,1,0:T(1,128)S(1)} %reshape.134), channel_id=1, replica_groups=mesh['row'=16,'col'=32] {'col'}, dimensions={0} | all-to-all | bytes 524288 | tf_op jit(solution)/shard_map/all_to_all | solution.py:67
  470.7 5.0 %all-to-all-start.12 = ((f32[32,1,64]{2,1,0:T(1,128)}), f32[32,1,64]{2,1,0:T(1,128)S(1)}, u32[]{:S(2)}, u32[]{:S(2)}) async-start(f32[32,1,64]{2,1,0:T(1,128)} %broadcast_in_dim.126), calls=%async_computation.12 | async-start | bytes 32768 | tf_op jit(solution)/shard_map/all_to_all | solution.py:9
  476.4 11.1 %all-to-all-done.12 = f32[32,1,64]{2,1,0:T(1,128)S(1)} async-done(((f32[32,1,64]{2,1,0:T(1,128)}), f32[32,1,64]{2,1,0:T(1,128)S(1)}, u32[]{:S(2)}, u32[]{:S(2)}) %all-to-all-start.12) | async-done | bytes 8224 | tf_op jit(solution)/shard_map/all_to_all | solution.py:9
  (381 shorter events, 189.5 us)
Async XLA Ops:
  119.5 27.1 %all-to-all-start.2 = ((f32[32,1,2048]{2,1,0:T(1,128)}), f32[32,1,2048]{2,1,0:T(1,128)S(1)}, u32[]{:S(2)}, u32[]{:S(2)}) async-start(f32[32,1,2048]{2,1,0:T(1,128)} %reshape.116), calls=%async_computation.2 | async-start | bytes 524288 | tf_op jit(solution)/shard_map/all_to_all | solution.py:67
  231.2 28.2 %all-to-all-start.5 = ((f32[32,1,2048]{2,1,0:T(1,128)}), f32[32,1,2048]{2,1,0:T(1,128)S(1)}, u32[]{:S(2)}, u32[]{:S(2)}) async-start(f32[32,1,2048]{2,1,0:T(1,128)} %reshape.122), calls=%async_computation.5 | async-start | bytes 524288 | tf_op jit(solution)/shard_map/all_to_all | solution.py:67
  343.9 28.0 %all-to-all-start.8 = ((f32[32,1,2048]{2,1,0:T(1,128)}), f32[32,1,2048]{2,1,0:T(1,128)S(1)}, u32[]{:S(2)}, u32[]{:S(2)}) async-start(f32[32,1,2048]{2,1,0:T(1,128)} %reshape.128), calls=%async_computation.8 | async-start | bytes 524288 | tf_op jit(solution)/shard_map/all_to_all | solution.py:67
  470.7 16.9 %all-to-all-start.12 = ((f32[32,1,64]{2,1,0:T(1,128)}), f32[32,1,64]{2,1,0:T(1,128)S(1)}, u32[]{:S(2)}, u32[]{:S(2)}) async-start(f32[32,1,64]{2,1,0:T(1,128)} %broadcast_in_dim.126), calls=%async_computation.12 | async-start | bytes 32768 | tf_op jit(solution)/shard_map/all_to_all | solution.py:9
where the time goes:
time: 491 us; the launch traced here: 488 us
  blocking collectives  186 us (38%)
  other arithmetic  124 us (25%)
  waiting for transfers between devices  76 us (15%)
  local copies, waits for them, and re-layouts  74 us (15%)
  starting transfers between devices  23.4 us (5%)
    all_to_all x4, blocking collectives, shards(): lax.all_to_all(shaped, 'col', split_axis=1, concat_axis=1, tiled=True)  116 us
    reduce_max x64, other arithmetic, step(): jnp.max(part_a[:, :, None] + part_d[None, :, :], axis=1)  98.3 us
    all_to_all x3, waiting for transfers between devices, shards(): lax.all_to_all(outgoing, 'col', split_axis=0, concat_axis=0, tiled=True)  64.9 us
    dynamic_slice x64, local copies, waits for them, and re-layouts, step(): part_d = lax.dynamic_slice_in_dim(masked, start, width, 0)  44.4 us
    all_to_all x4, blocking collectives, from_everyone(): return lax.all_to_all(copies, axis, split_axis=0, concat_axis=0, tiled=True)  43.1 us
    all_to_all x1, blocking collectives, shards(): lax.all_to_all(outgoing, 'col', split_axis=0, concat_axis=0, tiled=True)  27.1 us
    all_to_all x3, starting transfers between devices, shards(): lax.all_to_all(outgoing, 'col', split_axis=0, concat_axis=0, tiled=True)  18.4 us
    dynamic_slice x112, local copies, waits for them, and re-layouts, step(): part_a = lax.dynamic_slice_in_dim(times, start, width, 1)  17.8 us
  transfers between devices with their start and end apart: 4, of which 4 were waited for; matrix products, arithmetic and copies ran while one was open for 0% of the time, Pallas kernels for 0%

commit v1 on v0

v1 whole, which is shorter than its diff:
```python
import functools

import jax
import jax.numpy as jnp
import numpy as np
from jax import lax
from jax.experimental import pallas as pl
from jax.experimental.pallas import tpu as pltpu
from jax.sharding import Mesh
from jax.sharding import PartitionSpec as P

SUB, LANE = 8, 128
EMPTY = -1000000000.0
CHUNKS = 4
STEP = 8


def level_kernel(level, flags_ref, t_ref, delay_ref, out_ref, raw, wide, sems):
    rows, width = wide.shape
    groups, tiles = t_ref.shape[0], t_ref.shape[1]
    part = rows // CHUNKS
    half = width // 2

    def fetch(chunk):
        span = pl.ds(chunk * part, part)
        return pltpu.make_async_copy(delay_ref.at[level, span, :], raw.at[span, :], sems.at[chunk])

    for chunk in range(CHUNKS):
        fetch(chunk).start()
    out_ref[...] = jnp.full(out_ref.shape, EMPTY, jnp.float32)
    for chunk in range(CHUNKS):
        fetch(chunk).wait()
        span = pl.ds(chunk * part, part)
        for side in range(2):
            cols = slice(side * half, (side + 1) * half)
            value = raw[span, cols].astype(jnp.float32)
            wide[span, cols] = jnp.where(flags_ref[side] > 0, value, jnp.float32(EMPTY))
        tile = chunk
        for block in range(2):
            base = block * (groups // 2)
            n = groups // 2
            lanes = width // LANE

            def step(index, carry):
                held, best = carry
                best = list(best)
                start = chunk * part + index * STEP
                for i in range(STEP):
                    row = jnp.broadcast_to(wide[pl.ds(start + i, 1), :], (SUB, width))
                    for g in range(n):
                        value = jnp.broadcast_to(held[g][:, i : i + 1], (SUB, LANE))
                        for j in range(lanes):
                            k = g * lanes + j
                            best[k] = jnp.maximum(best[k], value + row[:, j * LANE : (j + 1) * LANE])
                held = tuple(pltpu.roll(h, LANE - STEP, 1) for h in held)
                return held, tuple(best)

            held = tuple(t_ref[base + g, tile] for g in range(n))
            place = lambda g, j: (base + g, (j % 4) // 2, j // 4, j % 2)
            best = tuple(out_ref[place(g, j)] for g in range(n) for j in range(lanes))
            held, best = lax.fori_loop(0, part // STEP, step, (held, best))
            for g in range(n):
                for j in range(lanes):
                    out_ref[place(g, j)] = best[g * lanes + j]


def level_max(level, flags, times, delay):
    rows, width = delay.shape[1:]
    groups = times.shape[0]
    work = times.shape[0] * SUB * rows * width
    return pl.pallas_call(
        functools.partial(level_kernel, level),
        out_shape=jax.ShapeDtypeStruct((groups, 2, 2, 2, SUB, LANE), jnp.float32),
        in_specs=[
            pl.BlockSpec(memory_space=pltpu.SMEM),
            pl.BlockSpec(memory_space=pltpu.VMEM),
            pl.BlockSpec(memory_space=pl.ANY),
        ],
        out_specs=pl.BlockSpec(memory_space=pltpu.VMEM),
        scratch_shapes=[
            pltpu.VMEM((rows, width), jnp.bfloat16),
            pltpu.VMEM((rows, width), jnp.float32),
            pltpu.SemaphoreType.DMA((CHUNKS,)),
        ],
        compiler_params=pltpu.CompilerParams(vmem_limit_bytes=16 * 1024 * 1024),
        cost_estimate=pl.CostEstimate(flops=2 * work, bytes_accessed=2 * rows * width, transcendentals=0),
        name="level_max",
    )(flags, times, delay)


def exchange(value, axes):
    return lax.all_to_all(value, axes, split_axis=0, concat_axis=0, tiled=True)


def shards(arrival, delay, occupancy):
    scenarios, pins = arrival.shape
    levels = delay.shape[0]
    plane = lax.axis_size("x") * lax.axis_size("y")
    place = lax.axis_index("x") * lax.axis_size("y") + lax.axis_index("y")
    col = lax.axis_index("z") * lax.axis_size("k") + lax.axis_index("k")
    flags = lax.dynamic_slice(occupancy, (0, col, place * 2), (levels, 1, 2))[:, 0, :]
    groups, tiles = scenarios // SUB, pins // LANE
    times = jnp.transpose(arrival.reshape(groups, SUB, tiles, LANE), (0, 2, 1, 3))
    worst = None
    for level in range(levels):
        last = level == levels - 1
        best = level_max(level, flags[level], times, delay)
        parts = best.reshape(plane * 2, 2, SUB, LANE)
        if last:
            top = jnp.max(best, axis=(1, 2, 3))
            top = jnp.broadcast_to(jnp.max(top, axis=2)[:, :, None], (groups, SUB, LANE))
            top = jnp.max(jnp.where(lax.broadcasted_iota(jnp.int32, (groups, SUB, LANE), 2) == lax.broadcasted_iota(jnp.int32, (groups, SUB, LANE), 0), top, EMPTY), axis=0)
            parts = jnp.concatenate([parts, jnp.broadcast_to(top[None, None], (plane * 2, 1, SUB, LANE))], axis=1)
        got = exchange(parts, ("x", "y", "k"))
        got = got.reshape(plane, 2, *got.shape[1:])
        got = jnp.maximum(got[:, 0], got[:, 1])
        if last:
            top = jnp.max(got[:, 2], axis=0)
            got = jnp.concatenate([got[:, :2], jnp.broadcast_to(top[None, None], (plane, 1, SUB, LANE))], axis=1)
        got = jnp.max(exchange(got, "z"), axis=0)
        if last:
            worst = jnp.transpose(got[2, :, :groups]).reshape(scenarios)
            got = got[:2]
        whole = exchange(jnp.broadcast_to(got[None], (plane, 2, SUB, LANE)), ("x", "y"))
        times = whole.reshape(groups, tiles, SUB, LANE)
    final = jnp.transpose(times, (0, 2, 1, 3)).reshape(scenarios, pins)
    return (final, worst)


def solution(mesh):
    shape = (4, 4, mesh.shape["col"] // 2, 2)
    fine = Mesh(np.asarray(mesh.devices).reshape(shape), ("x", "y", "z", "k"))
    col = ("z", "k")
    placed = (P(None, col), P(None, col, ("x", "y")), P())
    return jax.shard_map(
        shards, mesh=fine, in_specs=placed, out_specs=(P(None, col), P()), check_vma=False
    )
```

time: 491 us -> 281 us (0.57)
  other arithmetic: 124 us -> 0.38 us
  Pallas kernels: 0 us -> 80.4 us
  waiting for transfers between devices: 76 us -> 5.95 us
  local copies, waits for them, and re-layouts: 74 us -> 12.5 us
  starting transfers between devices: 23.4 us -> 3.51 us
  blocking collectives: 186 us -> 173 us
    reduce_max x70 -> x7, other arithmetic: 99.1 us -> 0.27 us  [the longest x1 0.1 us: shards(): jnp.max(top, axis=2)[:, :, None]]
    pallas_call x0 -> x4, Pallas kernels: none -> 80.4 us  [level_max(): pl.pallas_call(functools.partial(level_kernel, level), out_shape=jax.Shap...]
    all_to_all x4 -> x1, waiting for transfers between devices: 76 us -> 5.95 us  [exchange(): return lax.all_to_all(value, axes, split_axis=0, concat_axis=0, tiled=True)]
    dynamic_slice x179 -> x0, local copies, waits for them, and re-layouts: 62.2 us -> none  [the longest x64 44.4 us: step(): part_d = lax.dynamic_slice_in_dim(masked, start, width, 0)]
    all_to_all x4 -> x1, starting transfers between devices: 23.4 us -> 3.51 us  [exchange(): return lax.all_to_all(value, axes, split_axis=0, concat_axis=0, tiled=True)]
    all_to_all x12 -> x0, other arithmetic: 13.9 us -> none  [the longest x4 5.03 us: shards(): lax.all_to_all(outgoing, 'col', split_axis=0, concat_axis=0, tiled=True)]
    all_to_all x9 -> x11, blocking collectives: 186 us -> 173 us  [exchange(): return lax.all_to_all(value, axes, split_axis=0, concat_axis=0, tiled=True)]
    max x64 -> x4, other arithmetic: 5.52 us -> 0.07 us  [shards(): got = jnp.maximum(got[:, 0], got[:, 1])]
  transfers between devices with their start and end apart: 4 -> 1, of which waited for: 4 -> 1; matrix products, arithmetic and copies ran while one was open for 0% -> 0% of each run, Pallas kernels for 0% -> 0%
where the time goes in v1:
time: 281 us; the launch traced here: 277 us
  blocking collectives  173 us (62%)
  Pallas kernels  80.4 us (29%)
  local copies, waits for them, and re-layouts  12.5 us (4%)
  waiting for transfers between devices  5.95 us (2%)
  starting transfers between devices  3.51 us (1%)
    all_to_all x11, blocking collectives, exchange(): return lax.all_to_all(value, axes, split_axis=0, concat_axis=0, tiled=True)  173 us
    pallas_call x4, Pallas kernels, level_max(): pl.pallas_call(functools.partial(level_kernel, level), out_shape=jax.Shap...  80.4 us
    unnamed x11, local copies, waits for them, and re-layouts  10.3 us
    all_to_all x1, waiting for transfers between devices, exchange(): return lax.all_to_all(value, axes, split_axis=0, concat_axis=0, tiled=True)  5.95 us
  transfers between devices with their start and end apart: 1, of which 1 were waited for; matrix products, arithmetic and copies ran while one was open for 0% of the time, Pallas kernels for 0%

profile of v1, /device:TPU:1, one launch (start us, length us, event | category | flops | bytes accessed | tf_op | source)
XLA Modules:
  0.0 277.1 jit_solution(7439327943160113587)
XLA Ops:
  0.6 0.8 dynamic-slice_bitcast_fusion
  1.5 2.2 copy-done
  3.7 0.9 copy-done.4
  4.6 20.1 %level_max.4 = f32[8,2,2,2,8,128]{5,4,3,2,1,0:T(8,128)S(1)} custom-call(s32[2]{0:T(128)S(1)} %get-tuple-element.2.flags_ref, f32[8,4,8,128]{3,2,1,0:T(8,128)S(1)} %bitcast.46, bf16[4,512,1024]{2,1,0:T(8,128)(2,1)S(1)} %copy-done), custom_call_target="tpu_custom_call" | custom-call | flops 67108864 | bytes 1048576 | tf_op jit(solution)/shard_map/level_max/pallas_call | solution.py:71
  24.7 18.5 %all_to_all.60 = f32[32,2,8,128]{3,2,1,0:T(8,128)S(1)} all-to-all(f32[32,2,8,128]{3,2,1,0:T(8,128)S(1)} %bitcast.42), channel_id=1, replica_groups=mesh['x'=4,'y'=4,'z'=16,'k'=2] {'x','y','k'}, dimensions={0} | all-to-all | bytes 524288 | tf_op jit(solution)/shard_map/all_to_all | solution.py:92
  43.2 25.6 %all_to_all.61 = f32[16,2,8,128]{3,2,1,0:T(8,128)S(1)} all-to-all(f32[16,2,8,128]{3,2,1,0:T(8,128)S(1)} %fusion.3), channel_id=1, replica_groups=mesh['x'=4,'y'=4,'z'=16,'k'=2] {'z'}, dimensions={0} | all-to-all | bytes 262144 | tf_op jit(solution)/shard_map/all_to_all | solution.py:92
  68.9 9.4 %all_to_all.62 = f32[16,2,8,128]{3,2,1,0:T(8,128)S(1)} all-to-all(f32[16,2,8,128]{3,2,1,0:T(8,128)S(1)} %broadcast_in_dim.18), channel_id=1, replica_groups=mesh['x'=4,'y'=4,'z'=16,'k'=2] {'x','y'}, dimensions={0} | all-to-all | bytes 262144 | tf_op jit(solution)/shard_map/all_to_all | solution.py:92
  78.3 2.2 copy-done.1
  80.5 20.1 %level_max.5 = f32[8,2,2,2,8,128]{5,4,3,2,1,0:T(8,128)S(1)} custom-call(s32[2]{0:T(128)S(1)} %get-tuple-element.3.flags_ref, f32[8,4,8,128]{3,2,1,0:T(8,128)S(1)} %bitcast.44, bf16[4,512,1024]{2,1,0:T(8,128)(2,1)S(1)} %copy-done.1), custom_call_target="tpu_custom_call" | custom-call | flops 67108864 | bytes 1048576 | tf_op jit(solution)/shard_map/level_max/pallas_call | solution.py:71
  100.6 17.0 %all_to_all.63 = f32[32,2,8,128]{3,2,1,0:T(8,128)S(1)} all-to-all(f32[32,2,8,128]{3,2,1,0:T(8,128)S(1)} %bitcast.40), channel_id=1, replica_groups=mesh['x'=4,'y'=4,'z'=16,'k'=2] {'x','y','k'}, dimensions={0} | all-to-all | bytes 524288 | tf_op jit(solution)/shard_map/all_to_all | solution.py:92
  117.7 15.9 %all_to_all.64 = f32[16,2,8,128]{3,2,1,0:T(8,128)S(1)} all-to-all(f32[16,2,8,128]{3,2,1,0:T(8,128)S(1)} %fusion.2), channel_id=1, replica_groups=mesh['x'=4,'y'=4,'z'=16,'k'=2] {'z'}, dimensions={0} | all-to-all | bytes 262144 | tf_op jit(solution)/shard_map/all_to_all | solution.py:92
  133.5 9.4 %all_to_all.65 = f32[16,2,8,128]{3,2,1,0:T(8,128)S(1)} all-to-all(f32[16,2,8,128]{3,2,1,0:T(8,128)S(1)} %broadcast_in_dim.19), channel_id=1, replica_groups=mesh['x'=4,'y'=4,'z'=16,'k'=2] {'x','y'}, dimensions={0} | all-to-all | bytes 262144 | tf_op jit(solution)/shard_map/all_to_all | solution.py:92
  143.0 2.2 copy-done.2
  145.2 20.1 %level_max.6 = f32[8,2,2,2,8,128]{5,4,3,2,1,0:T(8,128)S(1)} custom-call(s32[2]{0:T(128)S(1)} %get-tuple-element.4.flags_ref, f32[8,4,8,128]{3,2,1,0:T(8,128)S(1)} %bitcast.45, bf16[4,512,1024]{2,1,0:T(8,128)(2,1)S(1)} %copy-done.2), custom_call_target="tpu_custom_call" | custom-call | flops 67108864 | bytes 1048576 | tf_op jit(solution)/shard_map/level_max/pallas_call | solution.py:71
  165.3 17.0 %all_to_all.66 = f32[32,2,8,128]{3,2,1,0:T(8,128)S(1)} all-to-all(f32[32,2,8,128]{3,2,1,0:T(8,128)S(1)} %bitcast.41), channel_id=1, replica_groups=mesh['x'=4,'y'=4,'z'=16,'k'=2] {'x','y','k'}, dimensions={0} | all-to-all | bytes 524288 | tf_op jit(solution)/shard_map/all_to_all | solution.py:92
  182.3 15.9 %all_to_all.67 = f32[16,2,8,128]{3,2,1,0:T(8,128)S(1)} all-to-all(f32[16,2,8,128]{3,2,1,0:T(8,128)S(1)} %fusion.1), channel_id=1, replica_groups=mesh['x'=4,'y'=4,'z'=16,'k'=2] {'z'}, dimensions={0} | all-to-all | bytes 262144 | tf_op jit(solution)/shard_map/all_to_all | solution.py:92
  198.2 9.4 %all_to_all.68 = f32[16,2,8,128]{3,2,1,0:T(8,128)S(1)} all-to-all(f32[16,2,8,128]{3,2,1,0:T(8,128)S(1)} %broadcast_in_dim.20), channel_id=1, replica_groups=mesh['x'=4,'y'=4,'z'=16,'k'=2] {'x','y'}, dimensions={0} | all-to-all | bytes 262144 | tf_op jit(solution)/shard_map/all_to_all | solution.py:92
  207.6 2.2 copy-done.3
  209.8 20.1 %level_max.7 = f32[8,2,2,2,8,128]{5,4,3,2,1,0:T(8,128)S(1)} custom-call(s32[2]{0:T(128)S(1)} %get-tuple-element.5.flags_ref, f32[8,4,8,128]{3,2,1,0:T(8,128)S(1)} %bitcast.43, bf16[4,512,1024]{2,1,0:T(8,128)(2,1)S(1)} %copy-done.3), custom_call_target="tpu_custom_call" | custom-call | flops 67108864 | bytes 1048576 | tf_op jit(solution)/shard_map/level_max/pallas_call | solution.py:71
  230.2 18.3 %all_to_all.69 = f32[32,3,8,128]{3,2,1,0:T(8,128)S(1)} all-to-all(f32[32,3,8,128]{3,2,1,0:T(8,128)S(1)} %pad_maximum_fusion), channel_id=1, replica_groups=mesh['x'=4,'y'=4,'z'=16,'k'=2] {'x','y','k'}, dimensions={0} | all-to-all | bytes 786432 | tf_op jit(solution)/shard_map/all_to_all | solution.py:92
  248.6 17.0 %all_to_all.70 = f32[16,3,8,128]{3,2,1,0:T(8,128)S(1)} all-to-all(f32[16,3,8,128]{3,2,1,0:T(8,128)S(1)} %pad_maximum_fusion.1), channel_id=1, replica_groups=mesh['x'=4,'y'=4,'z'=16,'k'=2] {'z'}, dimensions={0} | all-to-all | bytes 393216 | tf_op jit(solution)/shard_map/all_to_all | solution.py:92
  265.6 0.7 broadcast_in_dim.25
  266.3 3.5 %all-to-all-start.11 = ((f32[16,2,8,128]{3,2,1,0:T(8,128)}), f32[16,2,8,128]{3,2,1,0:T(8,128)S(1)}, u32[]{:S(2)}, u32[]{:S(2)}) async-start(f32[16,2,8,128]{3,2,1,0:T(8,128)} %broadcast_in_dim.25), calls=%async_computation.11 | async-start | bytes 262144 | tf_op jit(solution)/shard_map/all_to_all | solution.py:92
  270.5 6.0 %all-to-all-done.11 = f32[16,2,8,128]{3,2,1,0:T(8,128)S(1)} async-done(((f32[16,2,8,128]{3,2,1,0:T(8,128)}), f32[16,2,8,128]{3,2,1,0:T(8,128)S(1)}, u32[]{:S(2)}, u32[]{:S(2)}) %all-to-all-start.11) | async-done | bytes 131104 | tf_op jit(solution)/shard_map/all_to_all | solution.py:92
  (29 shorter events, 1.8 us)
Async XLA Ops:
  1.5 2.2 copy-start
  3.7 0.9 copy-start.4
  78.3 2.2 copy-start.1
  143.0 2.2 copy-start.2
  207.6 2.2 copy-start.3
  266.3 10.2 %all-to-all-start.11 = ((f32[16,2,8,128]{3,2,1,0:T(8,128)}), f32[16,2,8,128]{3,2,1,0:T(8,128)S(1)}, u32[]{:S(2)}, u32[]{:S(2)}) async-start(f32[16,2,8,128]{3,2,1,0:T(8,128)} %broadcast_in_dim.25), calls=%async_computation.11 | async-start | bytes 262144 | tf_op jit(solution)/shard_map/all_to_all | solution.py:92

commit v2 on v1

v2 whole, which is shorter than its diff:
```python
import functools

import jax
import jax.numpy as jnp
import numpy as np
from jax import lax
from jax.experimental import pallas as pl
from jax.experimental.pallas import tpu as pltpu
from jax.sharding import Mesh
from jax.sharding import PartitionSpec as P

SUB, LANE = 8, 128
EMPTY = -1000000000.0
GROUPS = 8
LANES = 8
SHIFT = 8
TURNS = 4


def level_body(flags_ref, t_ref, delay_ref, out_ref, spread_a, spread_b, wide, turned):
    tiles = t_ref.shape[1]
    rotations = LANE // (SHIFT * TURNS)
    chunk = tiles * SHIFT

    for m in range(rotations):
        for tile in range(tiles):
            for g in range(GROUPS):
                value = t_ref[g, tile]
                turned[m, tile, g] = pltpu.roll(value, LANE - m * SHIFT * TURNS, 1) if m else value
    out_ref[...] = jnp.full(out_ref.shape, EMPTY, jnp.float32)

    def spread_one(dest, m, e, q, a, g, held):
        lane = e * SHIFT + a
        dest[q * SHIFT + a, g] = jnp.broadcast_to(held[g][:, lane : lane + 1], (SUB, LANE))

    def warm(q, _):
        held = [turned[0, q, g] for g in range(GROUPS)]
        for a in range(SHIFT):
            for g in range(GROUPS):
                spread_one(spread_a, 0, 0, q, a, g, held)
        rows = pl.ds(pl.multiple_of(q * LANE, LANE), LANE)
        for j in range(LANES):
            value = delay_ref[rows, j * LANE : (j + 1) * LANE].astype(jnp.float32)
            wide[j, rows, :] = jnp.where(flags_ref[j // 4] > 0, value, jnp.float32(EMPTY))
        return 0

    lax.fori_loop(0, tiles, warm, 0)

    def stage(m, e, source, dest):
        next_m = m if e + 1 < TURNS else jnp.minimum(m + 1, rotations - 1)
        next_e = (e + 1) % TURNS

        def body(q, _):
            gb = (q // 2) * 4
            side = q % 2
            held = [turned[next_m, q, g] for g in range(GROUPS)]
            keys = [(g, j) for g in range(4) for j in range(4)]
            best = {(g, j): out_ref[gb + g, j // 2, side, j % 2] for g, j in keys}
            todo = [(a, g) for a in range(SHIFT) for g in range(GROUPS)]
            for k in range(chunk):
                place = (k // SHIFT) * LANE + e * SHIFT + k % SHIFT
                at = pl.ds(m * (SHIFT * TURNS) + place, 1)
                row = [jnp.broadcast_to(wide[side * 4 + j, at, :], (SUB, LANE)) for j in range(4)]
                for g in range(4):
                    value = source[k, gb + g]
                    for j in range(4):
                        best[g, j] = jnp.maximum(best[g, j], value + row[j])
                for _ in range(2):
                    a, g = todo.pop(0)
                    spread_one(dest, next_m, next_e, q, a, g, held)
            for g, j in keys:
                out_ref[gb + g, j // 2, side, j % 2] = best[g, j]
            return 0

        lax.fori_loop(0, 4, body, 0)

    def rotation(m, _):
        for e in range(TURNS):
            pair = (spread_a, spread_b) if e % 2 == 0 else (spread_b, spread_a)
            stage(m, e, *pair)
        return 0

    lax.fori_loop(0, rotations, rotation, 0)


def first_kernel(flags_ref, t_ref, delay_ref, out_ref, later_ref, spread_a, spread_b, wide, turned, raw, sems):
    own = pltpu.make_async_copy(delay_ref.at[0], raw, sems.at[0])
    own.start()
    rest = pltpu.make_async_copy(delay_ref.at[pl.ds(1, later_ref.shape[0])], later_ref, sems.at[1])
    rest.start()
    own.wait()
    level_body(flags_ref, t_ref, raw, out_ref, spread_a, spread_b, wide, turned)
    rest.wait()


def later_kernel(level, flags_ref, t_ref, later_ref, out_ref, spread_a, spread_b, wide, turned):
    level_body(flags_ref, t_ref, later_ref.at[level - 1], out_ref, spread_a, spread_b, wide, turned)


def level_max(level, flags, times, delay):
    rows, width = delay.shape[1:]
    tiles = rows // LANE
    work = GROUPS * SUB * rows * width
    vmem = pl.BlockSpec(memory_space=pltpu.VMEM)
    shape = jax.ShapeDtypeStruct((GROUPS, 2, 2, 2, SUB, LANE), jnp.float32)
    scratch = [
        pltpu.VMEM((tiles * SHIFT, GROUPS, SUB, LANE), jnp.float32),
        pltpu.VMEM((tiles * SHIFT, GROUPS, SUB, LANE), jnp.float32),
        pltpu.VMEM((LANES, rows, LANE), jnp.float32),
        pltpu.VMEM((LANE // (SHIFT * TURNS), tiles, GROUPS, SUB, LANE), jnp.float32),
    ]
    common = dict(
        compiler_params=pltpu.CompilerParams(vmem_limit_bytes=16 * 1024 * 1024),
        cost_estimate=pl.CostEstimate(flops=2 * work, bytes_accessed=2 * rows * width, transcendentals=0),
    )
    smem = pl.BlockSpec(memory_space=pltpu.SMEM)
    if level == 0:
        rest = jax.ShapeDtypeStruct((delay.shape[0] - 1, rows, width), delay.dtype)
        return pl.pallas_call(
            first_kernel,
            out_shape=(shape, rest),
            in_specs=[smem, vmem, pl.BlockSpec(memory_space=pltpu.HBM)],
            out_specs=(vmem, vmem),
            scratch_shapes=scratch + [pltpu.VMEM((rows, width), delay.dtype), pltpu.SemaphoreType.DMA((2,))],
            name="first_level",
            **common,
        )(flags, times, delay)
    return pl.pallas_call(
        functools.partial(later_kernel, level),
        out_shape=shape,
        in_specs=[smem, vmem, vmem],
        out_specs=vmem,
        scratch_shapes=scratch,
        name="later_level",
        **common,
    )(flags, times, delay)


def exchange(value, axes):
    return lax.all_to_all(value, axes, split_axis=0, concat_axis=0, tiled=True)


def shards(arrival, delay, occupancy):
    scenarios, pins = arrival.shape
    levels = delay.shape[0]
    plane = lax.axis_size("x") * lax.axis_size("y")
    place = lax.axis_index("x") * lax.axis_size("y") + lax.axis_index("y")
    col = lax.axis_index("z") * lax.axis_size("k") + lax.axis_index("k")
    flags = lax.dynamic_slice(occupancy, (0, col, place * 2), (levels, 1, 2))[:, 0, :]
    groups, tiles = scenarios // SUB, pins // LANE
    times = jnp.transpose(arrival.reshape(groups, SUB, tiles, LANE), (0, 2, 1, 3))
    worst = None
    for level in range(levels):
        last = level == levels - 1
        if level == 0:
            best, later = level_max(level, flags[level], times, delay)
        else:
            best = level_max(level, flags[level], times, later)
        parts = best.reshape(plane * 2, 2, SUB, LANE)
        if last:
            top = jnp.max(best, axis=(1, 2, 3))
            top = jnp.broadcast_to(jnp.max(top, axis=2)[:, :, None], (groups, SUB, LANE))
            top = jnp.max(jnp.where(lax.broadcasted_iota(jnp.int32, (groups, SUB, LANE), 2) == lax.broadcasted_iota(jnp.int32, (groups, SUB, LANE), 0), top, EMPTY), axis=0)
            parts = jnp.concatenate([parts, jnp.broadcast_to(top[None, None], (plane * 2, 1, SUB, LANE))], axis=1)
        got = exchange(parts, ("x", "y", "k"))
        got = got.reshape(plane, 2, *got.shape[1:])
        got = jnp.maximum(got[:, 0], got[:, 1])
        if last:
            top = jnp.max(got[:, 2], axis=0)
            got = jnp.concatenate([got[:, :2], jnp.broadcast_to(top[None, None], (plane, 1, SUB, LANE))], axis=1)
        got = jnp.max(exchange(got, "z"), axis=0)
        if last:
            worst = jnp.transpose(got[2, :, :groups]).reshape(scenarios)
            got = got[:2]
        whole = exchange(jnp.broadcast_to(got[None], (plane, 2, SUB, LANE)), ("x", "y"))
        times = whole.reshape(groups, tiles, SUB, LANE)
    final = jnp.transpose(times, (0, 2, 1, 3)).reshape(scenarios, pins)
    return (final, worst)


def solution(mesh):
    shape = (4, 4, mesh.shape["col"] // 2, 2)
    fine = Mesh(np.asarray(mesh.devices).reshape(shape), ("x", "y", "z", "k"))
    col = ("z", "k")
    placed = (P(None, col), P(None, col, ("x", "y")), P())
    return jax.shard_map(
        shards, mesh=fine, in_specs=placed, out_specs=(P(None, col), P()), check_vma=False
    )
```

time: 281 us -> 239 us (0.85)
  Pallas kernels: 80.4 us -> 44.5 us
  local copies, waits for them, and re-layouts: 12.5 us -> 5.96 us
    pallas_call x4, Pallas kernels: 80.4 us -> 44.5 us  [the longest x3 33.1 us: level_max(): pl.pallas_call(functools.partial(later_kernel, level), out_shape=shape, i...]
    unnamed x11 -> x5, local copies, waits for them, and re-layouts: 10.3 us -> 3.75 us
where the time goes in v2:
time: 239 us; the launch traced here: 235 us
  blocking collectives  173 us (72%)
  Pallas kernels  44.5 us (19%)
  local copies, waits for them, and re-layouts  5.96 us (2%)
  waiting for transfers between devices  5.95 us (2%)
  starting transfers between devices  3.51 us (1%)
    all_to_all x11, blocking collectives, exchange(): return lax.all_to_all(value, axes, split_axis=0, concat_axis=0, tiled=True)  173 us
    pallas_call x3, Pallas kernels, level_max(): pl.pallas_call(functools.partial(later_kernel, level), out_shape=shape, i...  33.1 us
    pallas_call x1, Pallas kernels, level_max(): pl.pallas_call(first_kernel, out_shape=(shape, rest), in_specs=[smem, vme...  11.4 us
    all_to_all x1, waiting for transfers between devices, exchange(): return lax.all_to_all(value, axes, split_axis=0, concat_axis=0, tiled=True)  5.95 us
  transfers between devices with their start and end apart: 1, of which 1 were waited for; matrix products, arithmetic and copies ran while one was open for 0% of the time, Pallas kernels for 0%

profile of v2, /device:TPU:1, one launch (start us, length us, event | category | flops | bytes accessed | tf_op | source)
XLA Modules:
  0.0 234.6 jit_solution(2278406095286298051)
XLA Ops:
  0.6 0.8 dynamic-slice_bitcast_fusion
  1.5 2.2 copy-done
  3.7 0.9 copy-done.1
  4.6 11.4 %first_level.1 = (f32[8,2,2,2,8,128]{5,4,3,2,1,0:T(8,128)S(1)}, bf16[3,512,1024]{2,1,0:T(8,128)(2,1)S(1)}) custom-call(s32[2]{0:T(128)S(1)} %get-tuple-element.6.flags_ref, f32[8,4,8,128]{3,2,1,0:T(8,128)S(1)} %bitcast.46, bf16[4,512,1024]{2,1,0:T(8,128)(2,1)S(1)} %copy-done), custom_call_target="tpu_custom_call" | custom-call | flops 67108864 | bytes 1048576 | tf_op jit(solution)/shard_map/first_level/pallas_call | solution.py:119
  15.9 18.5 %all_to_all.60 = f32[32,2,8,128]{3,2,1,0:T(8,128)S(1)} all-to-all(f32[32,2,8,128]{3,2,1,0:T(8,128)S(1)} %bitcast.45), channel_id=1, replica_groups=mesh['x'=4,'y'=4,'z'=16,'k'=2] {'x','y','k'}, dimensions={0} | all-to-all | bytes 524288 | tf_op jit(solution)/shard_map/all_to_all | solution.py:140
  34.5 25.6 %all_to_all.61 = f32[16,2,8,128]{3,2,1,0:T(8,128)S(1)} all-to-all(f32[16,2,8,128]{3,2,1,0:T(8,128)S(1)} %fusion.3), channel_id=1, replica_groups=mesh['x'=4,'y'=4,'z'=16,'k'=2] {'z'}, dimensions={0} | all-to-all | bytes 262144 | tf_op jit(solution)/shard_map/all_to_all | solution.py:140
  60.2 9.4 %all_to_all.62 = f32[16,2,8,128]{3,2,1,0:T(8,128)S(1)} all-to-all(f32[16,2,8,128]{3,2,1,0:T(8,128)S(1)} %broadcast_in_dim.18), channel_id=1, replica_groups=mesh['x'=4,'y'=4,'z'=16,'k'=2] {'x','y'}, dimensions={0} | all-to-all | bytes 262144 | tf_op jit(solution)/shard_map/all_to_all | solution.py:140
  69.6 11.0 %later_level.3 = f32[8,2,2,2,8,128]{5,4,3,2,1,0:T(8,128)S(1)} custom-call(s32[2]{0:T(128)S(1)} %get-tuple-element.7.flags_ref, f32[8,4,8,128]{3,2,1,0:T(8,128)S(1)} %bitcast.43, bf16[3,512,1024]{2,1,0:T(8,128)(2,1)S(1)} %get-tuple-element.5.later_ref), custom_call_target="tpu_custom_call" | custom-call | flops 67108864 | bytes 1048576 | tf_op jit(solution)/shard_map/later_level/pallas_call | solution.py:128
  80.6 17.0 %all_to_all.63 = f32[32,2,8,128]{3,2,1,0:T(8,128)S(1)} all-to-all(f32[32,2,8,128]{3,2,1,0:T(8,128)S(1)} %bitcast.40), channel_id=1, replica_groups=mesh['x'=4,'y'=4,'z'=16,'k'=2] {'x','y','k'}, dimensions={0} | all-to-all | bytes 524288 | tf_op jit(solution)/shard_map/all_to_all | solution.py:140
  97.7 15.9 %all_to_all.64 = f32[16,2,8,128]{3,2,1,0:T(8,128)S(1)} all-to-all(f32[16,2,8,128]{3,2,1,0:T(8,128)S(1)} %fusion.2), channel_id=1, replica_groups=mesh['x'=4,'y'=4,'z'=16,'k'=2] {'z'}, dimensions={0} | all-to-all | bytes 262144 | tf_op jit(solution)/shard_map/all_to_all | solution.py:140
  113.5 9.4 %all_to_all.65 = f32[16,2,8,128]{3,2,1,0:T(8,128)S(1)} all-to-all(f32[16,2,8,128]{3,2,1,0:T(8,128)S(1)} %broadcast_in_dim.19), channel_id=1, replica_groups=mesh['x'=4,'y'=4,'z'=16,'k'=2] {'x','y'}, dimensions={0} | all-to-all | bytes 262144 | tf_op jit(solution)/shard_map/all_to_all | solution.py:140
  123.0 11.0 %later_level.4 = f32[8,2,2,2,8,128]{5,4,3,2,1,0:T(8,128)S(1)} custom-call(s32[2]{0:T(128)S(1)} %get-tuple-element.8.flags_ref, f32[8,4,8,128]{3,2,1,0:T(8,128)S(1)} %bitcast.44, bf16[3,512,1024]{2,1,0:T(8,128)(2,1)S(1)} %get-tuple-element.5.later_ref), custom_call_target="tpu_custom_call" | custom-call | flops 67108864 | bytes 1048576 | tf_op jit(solution)/shard_map/later_level/pallas_call | solution.py:128
  134.0 17.0 %all_to_all.66 = f32[32,2,8,128]{3,2,1,0:T(8,128)S(1)} all-to-all(f32[32,2,8,128]{3,2,1,0:T(8,128)S(1)} %bitcast.41), channel_id=1, replica_groups=mesh['x'=4,'y'=4,'z'=16,'k'=2] {'x','y','k'}, dimensions={0} | all-to-all | bytes 524288 | tf_op jit(solution)/shard_map/all_to_all | solution.py:140
  151.0 15.9 %all_to_all.67 = f32[16,2,8,128]{3,2,1,0:T(8,128)S(1)} all-to-all(f32[16,2,8,128]{3,2,1,0:T(8,128)S(1)} %fusion.1), channel_id=1, replica_groups=mesh['x'=4,'y'=4,'z'=16,'k'=2] {'z'}, dimensions={0} | all-to-all | bytes 262144 | tf_op jit(solution)/shard_map/all_to_all | solution.py:140
  166.9 9.4 %all_to_all.68 = f32[16,2,8,128]{3,2,1,0:T(8,128)S(1)} all-to-all(f32[16,2,8,128]{3,2,1,0:T(8,128)S(1)} %broadcast_in_dim.20), channel_id=1, replica_groups=mesh['x'=4,'y'=4,'z'=16,'k'=2] {'x','y'}, dimensions={0} | all-to-all | bytes 262144 | tf_op jit(solution)/shard_map/all_to_all | solution.py:140
  176.4 11.0 %later_level.5 = f32[8,2,2,2,8,128]{5,4,3,2,1,0:T(8,128)S(1)} custom-call(s32[2]{0:T(128)S(1)} %get-tuple-element.9.flags_ref, f32[8,4,8,128]{3,2,1,0:T(8,128)S(1)} %bitcast.42, bf16[3,512,1024]{2,1,0:T(8,128)(2,1)S(1)} %get-tuple-element.5.later_ref), custom_call_target="tpu_custom_call" | custom-call | flops 67108864 | bytes 1048576 | tf_op jit(solution)/shard_map/later_level/pallas_call | solution.py:128
  187.4 0.1 reduce_max.70
  187.7 18.3 %all_to_all.69 = f32[32,3,8,128]{3,2,1,0:T(8,128)S(1)} all-to-all(f32[32,3,8,128]{3,2,1,0:T(8,128)S(1)} %pad_maximum_fusion), channel_id=1, replica_groups=mesh['x'=4,'y'=4,'z'=16,'k'=2] {'x','y','k'}, dimensions={0} | all-to-all | bytes 786432 | tf_op jit(solution)/shard_map/all_to_all | solution.py:140
  206.1 17.0 %all_to_all.70 = f32[16,3,8,128]{3,2,1,0:T(8,128)S(1)} all-to-all(f32[16,3,8,128]{3,2,1,0:T(8,128)S(1)} %pad_maximum_fusion.1), channel_id=1, replica_groups=mesh['x'=4,'y'=4,'z'=16,'k'=2] {'z'}, dimensions={0} | all-to-all | bytes 393216 | tf_op jit(solution)/shard_map/all_to_all | solution.py:140
  223.1 0.7 broadcast_in_dim.25
  223.8 3.5 %all-to-all-start.11 = ((f32[16,2,8,128]{3,2,1,0:T(8,128)}), f32[16,2,8,128]{3,2,1,0:T(8,128)S(1)}, u32[]{:S(2)}, u32[]{:S(2)}) async-start(f32[16,2,8,128]{3,2,1,0:T(8,128)} %broadcast_in_dim.25), calls=%async_computation.11 | async-start | bytes 262144 | tf_op jit(solution)/shard_map/all_to_all | solution.py:140
  227.4 0.6 reshape.86
  227.9 6.0 %all-to-all-done.11 = f32[16,2,8,128]{3,2,1,0:T(8,128)S(1)} async-done(((f32[16,2,8,128]{3,2,1,0:T(8,128)}), f32[16,2,8,128]{3,2,1,0:T(8,128)S(1)}, u32[]{:S(2)}, u32[]{:S(2)}) %all-to-all-start.11) | async-done | bytes 131104 | tf_op jit(solution)/shard_map/all_to_all | solution.py:140
  233.9 0.7 copy.8
  (23 shorter events, 0.4 us)
Async XLA Ops:
  1.5 2.2 copy-start
  3.7 0.9 copy-start.1
  223.8 10.2 %all-to-all-start.11 = ((f32[16,2,8,128]{3,2,1,0:T(8,128)}), f32[16,2,8,128]{3,2,1,0:T(8,128)S(1)}, u32[]{:S(2)}, u32[]{:S(2)}) async-start(f32[16,2,8,128]{3,2,1,0:T(8,128)} %broadcast_in_dim.25), calls=%async_computation.11 | async-start | bytes 262144 | tf_op jit(solution)/shard_map/all_to_all | solution.py:140

commit v3 on v2

v3 whole, which is shorter than its diff:
```python
import functools

import jax
import jax.numpy as jnp
import numpy as np
from jax import lax
from jax.experimental import pallas as pl
from jax.experimental.pallas import tpu as pltpu
from jax.sharding import Mesh
from jax.sharding import PartitionSpec as P

SUB, LANE = 8, 128
EMPTY = -1000000000.0
HALF = 4
TILES = 4
SHIFT = 8
TURNS = 4


def half_body(times, convert, wide, out_ref, spread_a, spread_b, turned):
    rotations = LANE // (SHIFT * TURNS)
    chunk = TILES * SHIFT

    for m in range(rotations):
        for tile in range(TILES):
            for g in range(HALF):
                value = times(g, tile)
                turned[m, tile, g] = pltpu.roll(value, LANE - m * SHIFT * TURNS, 1) if m else value
    out_ref[...] = jnp.full(out_ref.shape, EMPTY, jnp.float32)

    def held_rows(m, q):
        return {(t, g): turned[m, q * 2 + t, g] for t in range(2) for g in range(HALF)}

    def spread_one(dest, e, q, place, held):
        a, t, g = place
        lane = e * SHIFT + a
        row = (q * 2 + t) * SHIFT + a
        dest[row, g] = jnp.broadcast_to(held[t, g][:, lane : lane + 1], (SUB, LANE))

    places = [(a, t, g) for a in range(SHIFT) for t in range(2) for g in range(HALF)]

    def warm(q, _):
        held = held_rows(0, q)
        for place in places:
            spread_one(spread_a, 0, q, place, held)
        convert(q)
        return 0

    lax.fori_loop(0, 2, warm, 0)

    def stage(m, e, source, dest):
        next_m = m if e + 1 < TURNS else jnp.minimum(m + 1, rotations - 1)
        next_e = (e + 1) % TURNS

        def body(side, _):
            held = held_rows(next_m, side)
            keys = [(g, j) for g in range(HALF) for j in range(4)]
            best = {(g, j): out_ref[g, j, side] for g, j in keys}
            todo = list(places)
            for k in range(chunk):
                place = (k // SHIFT) * LANE + e * SHIFT + k % SHIFT
                at = pl.ds(m * (SHIFT * TURNS) + place, 1)
                row = [jnp.broadcast_to(wide[side * 4 + j, at, :], (SUB, LANE)) for j in range(4)]
                for g in range(HALF):
                    value = source[k, g]
                    for j in range(4):
                        best[g, j] = jnp.maximum(best[g, j], value + row[j])
                for _ in range(2):
                    spread_one(dest, next_e, side, todo.pop(0), held)
            for g, j in keys:
                out_ref[g, j, side] = best[g, j]
            return 0

        lax.fori_loop(0, 2, body, 0)

    def rotation(m, _):
        for e in range(TURNS):
            pair = (spread_a, spread_b) if e % 2 == 0 else (spread_b, spread_a)
            stage(m, e, *pair)
        return 0

    lax.fori_loop(0, rotations, rotation, 0)


def times_of(t_ref, half):
    if len(t_ref.shape) == 4:
        return lambda g, tile: t_ref[half * HALF + g, tile]
    return lambda g, tile: t_ref[g, tile, half]


def sent_kernel(level, flags_ref, t_ref, delay_ref, out_ref, wide, *scratch):
    def convert(q):
        rows = pl.ds(pl.multiple_of(q * 2 * LANE, LANE), 2 * LANE)
        for j in range(8):
            value = delay_ref[level, rows, j * LANE : (j + 1) * LANE].astype(jnp.float32)
            wide[j, rows, :] = jnp.where(flags_ref[j // 4] > 0, value, jnp.float32(EMPTY))

    half_body(times_of(t_ref, flags_ref[2]), convert, wide, out_ref, *scratch)


def kept_kernel(flags_ref, t_ref, wide, out_ref, *scratch):
    half_body(times_of(t_ref, flags_ref[3]), lambda q: None, wide, out_ref, *scratch)


def half_max(level, flags, times, source, shape):
    levels, rows, width = shape
    work = HALF * SUB * rows * width
    vmem = pl.BlockSpec(memory_space=pltpu.VMEM)
    out = jax.ShapeDtypeStruct((HALF, 4, 2, SUB, LANE), jnp.float32)
    wide = jax.ShapeDtypeStruct((width // LANE, rows, LANE), jnp.float32)
    spread = pltpu.VMEM((TILES * SHIFT, HALF, SUB, LANE), jnp.float32)
    sent = level is not None
    return pl.pallas_call(
        functools.partial(sent_kernel, level) if sent else kept_kernel,
        out_shape=(out, wide) if sent else out,
        in_specs=[pl.BlockSpec(memory_space=pltpu.SMEM), vmem, vmem],
        out_specs=(vmem, vmem) if sent else vmem,
        scratch_shapes=[
            spread,
            spread,
            pltpu.VMEM((LANE // (SHIFT * TURNS), TILES, HALF, SUB, LANE), jnp.float32),
        ],
        compiler_params=pltpu.CompilerParams(vmem_limit_bytes=16 * 1024 * 1024),
        cost_estimate=pl.CostEstimate(flops=2 * work, bytes_accessed=2 * rows * width, transcendentals=0),
        name="sent_half" if sent else "kept_half",
    )(flags, times, source)


def exchange(value, axes):
    return lax.all_to_all(value, axes, split_axis=0, concat_axis=0, tiled=True)


def shards(arrival, delay, occupancy):
    scenarios, pins = arrival.shape
    levels = delay.shape[0]
    plane = lax.axis_size("x") * lax.axis_size("y")
    depth = lax.axis_size("z")
    place = lax.axis_index("x") * lax.axis_size("y") + lax.axis_index("y")
    odd = lax.axis_index("z") % 2
    col = lax.axis_index("z") * lax.axis_size("k") + lax.axis_index("k")
    flags = lax.dynamic_slice(occupancy, (0, col, place * 2), (levels, 1, 2))[:, 0, :]
    halves = jnp.broadcast_to(jnp.stack([1 - odd, odd])[None], (levels, 2))
    flags = jnp.concatenate([flags, halves], axis=1)
    groups, tiles = scenarios // SUB, pins // LANE
    neighbour = [(z, z ^ 1) for z in range(depth)]
    times = jnp.transpose(arrival.reshape(groups, SUB, tiles, LANE), (0, 2, 1, 3))
    worst = None
    for level in range(levels):
        last = level == levels - 1
        sent, wide = half_max(0 if level == 0 else level, flags[level], times, delay[:1] if level == 0 else delay, delay.shape)
        got = lax.ppermute(sent, "z", neighbour)
        kept = half_max(None, flags[level], times, wide, delay.shape)
        best = jnp.maximum(kept, got)
        parts = best.reshape(plane * 2, 1, SUB, LANE)
        if last:
            top = jnp.max(jnp.max(best, axis=(1, 2)), axis=2)
            spot = lax.broadcasted_iota(jnp.int32, (HALF, SUB, LANE), 0) + odd * HALF
            here = lax.broadcasted_iota(jnp.int32, (HALF, SUB, LANE), 2) == spot
            top = jnp.max(jnp.where(here, top[:, :, None], EMPTY), axis=0)
            parts = jnp.concatenate([parts, jnp.broadcast_to(top[None, None], parts.shape)], axis=1)
        got = exchange(parts, ("x", "y", "k"))
        got = got.reshape(plane, 2, *got.shape[1:])
        got = jnp.maximum(got[:, 0], got[:, 1])
        if last:
            top = jnp.max(got[:, 1], axis=0)
            got = jnp.concatenate([got[:, :1], jnp.broadcast_to(top[None, None], (plane, 1, SUB, LANE))], axis=1)
        got = exchange(got, "z")
        if last:
            worst = jnp.transpose(jnp.max(got[:, 1], axis=0)[:, :groups]).reshape(scenarios)
        got = jnp.max(got[:, 0].reshape(depth // 2, 2, SUB, LANE), axis=0)
        whole = exchange(jnp.broadcast_to(got[None], (plane, 2, SUB, LANE)), ("x", "y"))
        times = whole.reshape(HALF, tiles, 2, SUB, LANE)
    final = jnp.transpose(times, (2, 0, 3, 1, 4)).reshape(scenarios, pins)
    return (final, worst)


def solution(mesh):
    shape = (4, 4, mesh.shape["col"] // 2, 2)
    fine = Mesh(np.asarray(mesh.devices).reshape(shape), ("x", "y", "z", "k"))
    col = ("z", "k")
    placed = (P(None, col), P(None, col, ("x", "y")), P())
    return jax.shard_map(
        shards, mesh=fine, in_specs=placed, out_specs=(P(None, col), P()), check_vma=False
    )
```

time: 239 us -> 268 us (1.12)
  Pallas kernels: 44.5 us -> 78.2 us
  blocking collectives: 173 us -> 159 us
  starting transfers between devices: 3.51 us -> 16.1 us
    pallas_call x4 -> x8, Pallas kernels: 44.5 us -> 78.2 us  [half_max(): pl.pallas_call(functools.partial(sent_kernel, level) if sent else kept_ke...]
    all_to_all x11, blocking collectives: 173 us -> 159 us  [exchange(): return lax.all_to_all(value, axes, split_axis=0, concat_axis=0, tiled=True)]
    ppermute x0 -> x4, starting transfers between devices: none -> 12.6 us  [shards(): got = lax.ppermute(sent, 'z', neighbour)]
    unnamed x5 -> x6, local copies, waits for them, and re-layouts: 3.75 us -> 0.67 us
  transfers between devices with their start and end apart: 1 -> 5, of which waited for: 1 -> 1; matrix products, arithmetic and copies ran while one was open for 0% -> 0% of each run, Pallas kernels for 0% -> 15%
where the time goes in v3:
time: 268 us; the launch traced here: 265 us
  blocking collectives  159 us (59%)
  Pallas kernels  78.2 us (29%)
  starting transfers between devices  16.1 us (6%)
  waiting for transfers between devices  5.94 us (2%)
  local copies, waits for them, and re-layouts  4.49 us (2%)
    all_to_all x11, blocking collectives, exchange(): return lax.all_to_all(value, axes, split_axis=0, concat_axis=0, tiled=True)  159 us
    pallas_call x8, Pallas kernels, half_max(): pl.pallas_call(functools.partial(sent_kernel, level) if sent else kept_ke...  78.2 us
    ppermute x4, starting transfers between devices, shards(): got = lax.ppermute(sent, 'z', neighbour)  12.6 us
    all_to_all x1, waiting for transfers between devices, exchange(): return lax.all_to_all(value, axes, split_axis=0, concat_axis=0, tiled=True)  5.93 us
  transfers between devices with their start and end apart: 5, of which 1 were waited for; matrix products, arithmetic and copies ran while one was open for 0% of the time, Pallas kernels for 15%

profile of v3, /device:TPU:1, one launch (start us, length us, event | category | flops | bytes accessed | tf_op | source)
XLA Modules:
  0.0 265.1 jit_solution(6831498948727050889)
XLA Ops:
  3.3 9.8 %sent_half.4 = (f32[4,4,2,8,128]{4,3,2,1,0:T(8,128)S(1)}, f32[8,512,128]{2,1,0:T(8,128)S(1)}) custom-call(s32[4]{0:T(128)S(1)} %get-tuple-element.18.flags_ref, f32[8,4,8,128]{3,2,1,0:T(8,128)S(1)} %bitcast.101, bf16[1,512,1024]{2,1,0:T(8,128)(2,1)S(1)} %slice.62.delay_ref), custom_call_target="tpu_custom_call" | custom-call | flops 33554432 | bytes 1048576 | tf_op jit(solution)/shard_map/sent_half/pallas_call | solution.py:113
  13.1 4.4 %collective-permute-start = (f32[4,4,2,8,128]{4,3,2,1,0:T(8,128)S(1)}, f32[4,4,2,8,128]{4,3,2,1,0:T(8,128)S(1)}, u32[]{:S(2)}, u32[]{:S(2)}) collective-permute-start(f32[4,4,2,8,128]{4,3,2,1,0:T(8,128)S(1)} %get-tuple-element.11), channel_id=1, source_target_pairs={{0,2},{2,0},{4,6},{6,4},{8,10},{10,8},{12,14},{14,12},{16,18},{18,... | collective-permute-start | bytes 393224 | tf_op jit(solution)/shard_map/ppermute | solution.py:151
  17.4 9.7 %kept_half.4 = f32[4,4,2,8,128]{4,3,2,1,0:T(8,128)S(1)} custom-call(s32[4]{0:T(128)S(1)} %get-tuple-element.18.flags_ref, f32[8,4,8,128]{3,2,1,0:T(8,128)S(1)} %bitcast.102, f32[8,512,128]{2,1,0:T(8,128)S(1)} %get-tuple-element.10.wide), custom_call_target="tpu_custom_call" | custom-call | flops 33554432 | bytes 1048576 | tf_op jit(solution)/shard_map/kept_half/pallas_call | solution.py:113
  27.2 15.5 %all_to_all.60 = f32[32,1,8,128]{3,2,1,0:T(8,128)S(1)} all-to-all(f32[32,1,8,128]{3,2,1,0:T(8,128)S(1)} %bitcast.104), channel_id=1, replica_groups=mesh['x'=4,'y'=4,'z'=16,'k'=2] {'x','y','k'}, dimensions={0} | all-to-all | bytes 262144 | tf_op jit(solution)/shard_map/all_to_all | solution.py:130
  42.7 25.4 %all_to_all.61 = f32[16,1,8,128]{3,2,1,0:T(8,128)S(1)} all-to-all(f32[16,1,8,128]{3,2,1,0:T(8,128)S(1)} %fusion.8), channel_id=1, replica_groups=mesh['x'=4,'y'=4,'z'=16,'k'=2] {'z'}, dimensions={0} | all-to-all | bytes 131072 | tf_op jit(solution)/shard_map/all_to_all | solution.py:130
  68.2 9.4 %all_to_all.62 = f32[16,2,8,128]{3,2,1,0:T(8,128)S(1)} all-to-all(f32[16,2,8,128]{3,2,1,0:T(8,128)S(1)} %broadcast_in_dim.27), channel_id=1, replica_groups=mesh['x'=4,'y'=4,'z'=16,'k'=2] {'x','y'}, dimensions={0} | all-to-all | bytes 262144 | tf_op jit(solution)/shard_map/all_to_all | solution.py:130
  77.6 9.8 %sent_half.5 = (f32[4,4,2,8,128]{4,3,2,1,0:T(8,128)S(1)}, f32[8,512,128]{2,1,0:T(8,128)S(1)}) custom-call(s32[4]{0:T(128)S(1)} %get-tuple-element.19.flags_ref, f32[4,4,2,8,128]{4,3,2,1,0:T(8,128)S(1)} %bitcast.97, bf16[4,512,1024]{2,1,0:T(8,128)(2,1)S(1)} %copy-done.1), custom_call_target="tpu_custom_call" | custom-call | flops 33554432 | bytes 1048576 | tf_op jit(solution)/shard_map/sent_half/pallas_call | solution.py:113
  87.4 2.7 %collective-permute-start.1 = (f32[4,4,2,8,128]{4,3,2,1,0:T(8,128)S(1)}, f32[4,4,2,8,128]{4,3,2,1,0:T(8,128)S(1)}, u32[]{:S(2)}, u32[]{:S(2)}) collective-permute-start(f32[4,4,2,8,128]{4,3,2,1,0:T(8,128)S(1)} %get-tuple-element.13), channel_id=1, source_target_pairs={{0,2},{2,0},{4,6},{6,4},{8,10},{10,8},{12,14},{14,12},{16,18},{18,... | collective-permute-start | bytes 393224 | tf_op jit(solution)/shard_map/ppermute | solution.py:151
  90.2 9.7 %kept_half.5 = f32[4,4,2,8,128]{4,3,2,1,0:T(8,128)S(1)} custom-call(s32[4]{0:T(128)S(1)} %get-tuple-element.19.flags_ref, f32[4,4,2,8,128]{4,3,2,1,0:T(8,128)S(1)} %bitcast.98, f32[8,512,128]{2,1,0:T(8,128)S(1)} %get-tuple-element.12.wide), custom_call_target="tpu_custom_call" | custom-call | flops 33554432 | bytes 1048576 | tf_op jit(solution)/shard_map/kept_half/pallas_call | solution.py:113
  99.9 14.8 %all_to_all.63 = f32[32,1,8,128]{3,2,1,0:T(8,128)S(1)} all-to-all(f32[32,1,8,128]{3,2,1,0:T(8,128)S(1)} %bitcast.105), channel_id=1, replica_groups=mesh['x'=4,'y'=4,'z'=16,'k'=2] {'x','y','k'}, dimensions={0} | all-to-all | bytes 262144 | tf_op jit(solution)/shard_map/all_to_all | solution.py:130
  114.8 14.5 %all_to_all.64 = f32[16,1,8,128]{3,2,1,0:T(8,128)S(1)} all-to-all(f32[16,1,8,128]{3,2,1,0:T(8,128)S(1)} %fusion.6), channel_id=1, replica_groups=mesh['x'=4,'y'=4,'z'=16,'k'=2] {'z'}, dimensions={0} | all-to-all | bytes 131072 | tf_op jit(solution)/shard_map/all_to_all | solution.py:130
  129.3 9.4 %all_to_all.65 = f32[16,2,8,128]{3,2,1,0:T(8,128)S(1)} all-to-all(f32[16,2,8,128]{3,2,1,0:T(8,128)S(1)} %broadcast_in_dim.28), channel_id=1, replica_groups=mesh['x'=4,'y'=4,'z'=16,'k'=2] {'x','y'}, dimensions={0} | all-to-all | bytes 262144 | tf_op jit(solution)/shard_map/all_to_all | solution.py:130
  138.7 9.8 %sent_half.6 = (f32[4,4,2,8,128]{4,3,2,1,0:T(8,128)S(1)}, f32[8,512,128]{2,1,0:T(8,128)S(1)}) custom-call(s32[4]{0:T(128)S(1)} %get-tuple-element.20.flags_ref, f32[4,4,2,8,128]{4,3,2,1,0:T(8,128)S(1)} %bitcast.99, bf16[4,512,1024]{2,1,0:T(8,128)(2,1)S(1)} %copy-done.1), custom_call_target="tpu_custom_call" | custom-call | flops 33554432 | bytes 1048576 | tf_op jit(solution)/shard_map/sent_half/pallas_call | solution.py:113
  148.5 2.7 %collective-permute-start.2 = (f32[4,4,2,8,128]{4,3,2,1,0:T(8,128)S(1)}, f32[4,4,2,8,128]{4,3,2,1,0:T(8,128)S(1)}, u32[]{:S(2)}, u32[]{:S(2)}) collective-permute-start(f32[4,4,2,8,128]{4,3,2,1,0:T(8,128)S(1)} %get-tuple-element.15), channel_id=1, source_target_pairs={{0,2},{2,0},{4,6},{6,4},{8,10},{10,8},{12,14},{14,12},{16,18},{18,... | collective-permute-start | bytes 393224 | tf_op jit(solution)/shard_map/ppermute | solution.py:151
  151.3 9.7 %kept_half.6 = f32[4,4,2,8,128]{4,3,2,1,0:T(8,128)S(1)} custom-call(s32[4]{0:T(128)S(1)} %get-tuple-element.20.flags_ref, f32[4,4,2,8,128]{4,3,2,1,0:T(8,128)S(1)} %bitcast.100, f32[8,512,128]{2,1,0:T(8,128)S(1)} %get-tuple-element.14.wide), custom_call_target="tpu_custom_call" | custom-call | flops 33554432 | bytes 1048576 | tf_op jit(solution)/shard_map/kept_half/pallas_call | solution.py:113
  161.1 14.8 %all_to_all.66 = f32[32,1,8,128]{3,2,1,0:T(8,128)S(1)} all-to-all(f32[32,1,8,128]{3,2,1,0:T(8,128)S(1)} %bitcast.106), channel_id=1, replica_groups=mesh['x'=4,'y'=4,'z'=16,'k'=2] {'x','y','k'}, dimensions={0} | all-to-all | bytes 262144 | tf_op jit(solution)/shard_map/all_to_all | solution.py:130
  175.9 14.5 %all_to_all.67 = f32[16,1,8,128]{3,2,1,0:T(8,128)S(1)} all-to-all(f32[16,1,8,128]{3,2,1,0:T(8,128)S(1)} %fusion.4), channel_id=1, replica_groups=mesh['x'=4,'y'=4,'z'=16,'k'=2] {'z'}, dimensions={0} | all-to-all | bytes 131072 | tf_op jit(solution)/shard_map/all_to_all | solution.py:130
  190.4 9.4 %all_to_all.68 = f32[16,2,8,128]{3,2,1,0:T(8,128)S(1)} all-to-all(f32[16,2,8,128]{3,2,1,0:T(8,128)S(1)} %broadcast_in_dim.29), channel_id=1, replica_groups=mesh['x'=4,'y'=4,'z'=16,'k'=2] {'x','y'}, dimensions={0} | all-to-all | bytes 262144 | tf_op jit(solution)/shard_map/all_to_all | solution.py:130
  199.8 9.8 %sent_half.7 = (f32[4,4,2,8,128]{4,3,2,1,0:T(8,128)S(1)}, f32[8,512,128]{2,1,0:T(8,128)S(1)}) custom-call(s32[4]{0:T(128)S(1)} %get-tuple-element.21.flags_ref, f32[4,4,2,8,128]{4,3,2,1,0:T(8,128)S(1)} %bitcast.95, bf16[4,512,1024]{2,1,0:T(8,128)(2,1)S(1)} %copy-done.1), custom_call_target="tpu_custom_call" | custom-call | flops 33554432 | bytes 1048576 | tf_op jit(solution)/shard_map/sent_half/pallas_call | solution.py:113
  212.4 9.7 %kept_half.7 = f32[4,4,2,8,128]{4,3,2,1,0:T(8,128)S(1)} custom-call(s32[4]{0:T(128)S(1)} %get-tuple-element.21.flags_ref, f32[4,4,2,8,128]{4,3,2,1,0:T(8,128)S(1)} %bitcast.96, f32[8,512,128]{2,1,0:T(8,128)S(1)} %get-tuple-element.16.wide), custom_call_target="tpu_custom_call" | custom-call | flops 33554432 | bytes 1048576 | tf_op jit(solution)/shard_map/kept_half/pallas_call | solution.py:113
  222.4 16.1 %all_to_all.69 = f32[32,2,8,128]{3,2,1,0:T(8,128)S(1)} all-to-all(f32[32,2,8,128]{3,2,1,0:T(8,128)S(1)} %pad_maximum_fusion), channel_id=1, replica_groups=mesh['x'=4,'y'=4,'z'=16,'k'=2] {'x','y','k'}, dimensions={0} | all-to-all | bytes 524288 | tf_op jit(solution)/shard_map/all_to_all | solution.py:130
  238.6 15.0 %all_to_all.70 = f32[16,2,8,128]{3,2,1,0:T(8,128)S(1)} all-to-all(f32[16,2,8,128]{3,2,1,0:T(8,128)S(1)} %pad_maximum_fusion.1), channel_id=1, replica_groups=mesh['x'=4,'y'=4,'z'=16,'k'=2] {'z'}, dimensions={0} | all-to-all | bytes 262144 | tf_op jit(solution)/shard_map/all_to_all | solution.py:130
  254.3 3.5 %all-to-all-start.11 = ((f32[16,2,8,128]{3,2,1,0:T(8,128)}), f32[16,2,8,128]{3,2,1,0:T(8,128)S(1)}, u32[]{:S(2)}, u32[]{:S(2)}) async-start(f32[16,2,8,128]{3,2,1,0:T(8,128)} %broadcast_in_dim.34), calls=%async_computation.11 | async-start | bytes 262144 | tf_op jit(solution)/shard_map/all_to_all | solution.py:130
  258.5 5.9 %all-to-all-done.11 = f32[16,2,8,128]{3,2,1,0:T(8,128)S(1)} async-done(((f32[16,2,8,128]{3,2,1,0:T(8,128)}), f32[16,2,8,128]{3,2,1,0:T(8,128)S(1)}, u32[]{:S(2)}, u32[]{:S(2)}) %all-to-all-start.11) | async-done | bytes 131104 | tf_op jit(solution)/shard_map/all_to_all | solution.py:130
  (47 shorter events, 7.8 us)
Async XLA Ops:
  0.6 0.8 copy-start
  0.6 2.6 copy-start.2
  3.3 74.4 %copy-start.1 = (bf16[4,512,1024]{2,1,0:T(8,128)(2,1)S(1)}, bf16[4,512,1024]{2,1,0:T(8,128)(2,1)}, u32[]{:S(2)}) copy-start(bf16[4,512,1024]{2,1,0:T(8,128)(2,1)} %delay_ref.5) | copy-start | bytes 12582916
  13.1 14.1 %collective-permute-start = (f32[4,4,2,8,128]{4,3,2,1,0:T(8,128)S(1)}, f32[4,4,2,8,128]{4,3,2,1,0:T(8,128)S(1)}, u32[]{:S(2)}, u32[]{:S(2)}) collective-permute-start(f32[4,4,2,8,128]{4,3,2,1,0:T(8,128)S(1)} %get-tuple-element.11), channel_id=1, source_target_pairs={{0,2},{2,0},{4,6},{6,4},{8,10},{10,8},{12,14},{14,12},{16,18},{18,... | collective-permute-start | bytes 393224 | tf_op jit(solution)/shard_map/ppermute | solution.py:151
  87.4 12.5 %collective-permute-start.1 = (f32[4,4,2,8,128]{4,3,2,1,0:T(8,128)S(1)}, f32[4,4,2,8,128]{4,3,2,1,0:T(8,128)S(1)}, u32[]{:S(2)}, u32[]{:S(2)}) collective-permute-start(f32[4,4,2,8,128]{4,3,2,1,0:T(8,128)S(1)} %get-tuple-element.13), channel_id=1, source_target_pairs={{0,2},{2,0},{4,6},{6,4},{8,10},{10,8},{12,14},{14,12},{16,18},{18,... | collective-permute-start | bytes 393224 | tf_op jit(solution)/shard_map/ppermute | solution.py:151
  148.5 12.5 %collective-permute-start.2 = (f32[4,4,2,8,128]{4,3,2,1,0:T(8,128)S(1)}, f32[4,4,2,8,128]{4,3,2,1,0:T(8,128)S(1)}, u32[]{:S(2)}, u32[]{:S(2)}) collective-permute-start(f32[4,4,2,8,128]{4,3,2,1,0:T(8,128)S(1)} %get-tuple-element.15), channel_id=1, source_target_pairs={{0,2},{2,0},{4,6},{6,4},{8,10},{10,8},{12,14},{14,12},{16,18},{18,... | collective-permute-start | bytes 393224 | tf_op jit(solution)/shard_map/ppermute | solution.py:151
  209.7 12.5 %collective-permute-start.3 = (f32[4,4,2,8,128]{4,3,2,1,0:T(8,128)S(1)}, f32[4,4,2,8,128]{4,3,2,1,0:T(8,128)S(1)}, u32[]{:S(2)}, u32[]{:S(2)}) collective-permute-start(f32[4,4,2,8,128]{4,3,2,1,0:T(8,128)S(1)} %get-tuple-element.17), channel_id=1, source_target_pairs={{0,2},{2,0},{4,6},{6,4},{8,10},{10,8},{12,14},{14,12},{16,18},{18,... | collective-permute-start | bytes 393224 | tf_op jit(solution)/shard_map/ppermute | solution.py:151
  254.3 10.2 %all-to-all-start.11 = ((f32[16,2,8,128]{3,2,1,0:T(8,128)}), f32[16,2,8,128]{3,2,1,0:T(8,128)S(1)}, u32[]{:S(2)}, u32[]{:S(2)}) async-start(f32[16,2,8,128]{3,2,1,0:T(8,128)} %broadcast_in_dim.34), calls=%async_computation.11 | async-start | bytes 262144 | tf_op jit(solution)/shard_map/all_to_all | solution.py:130

commit v4 on v3

--- a/solution.py
+++ b/solution.py
@@ -46,14 +46,17 @@
         convert(q)
         return 0
 
-    lax.fori_loop(0, 2, warm, 0)
+    for q in range(2):
+        warm(q, 0)
 
     def stage(m, e, source, dest):
         next_m = m if e + 1 < TURNS else jnp.minimum(m + 1, rotations - 1)
         next_e = (e + 1) % TURNS
 
-        def body(side, _):
-            held = held_rows(next_m, side)
+        def body(q, _):
+            side = lax.rem(q, 2)
+            late = (q // 2) * HALF
+            held = held_rows(next_m, q)
             keys = [(g, j) for g in range(HALF) for j in range(4)]
             best = {(g, j): out_ref[g, j, side] for g, j in keys}
             todo = list(places)
@@ -62,11 +65,11 @@
                 at = pl.ds(m * (SHIFT * TURNS) + place, 1)
                 row = [jnp.broadcast_to(wide[side * 4 + j, at, :], (SUB, LANE)) for j in range(4)]
                 for g in range(HALF):
-                    value = source[k, g]
+                    value = source[k, late + g]
                     for j in range(4):
                         best[g, j] = jnp.maximum(best[g, j], value + row[j])
                 for _ in range(2):
-                    spread_one(dest, next_e, side, todo.pop(0), held)
+                    spread_one(dest, next_e, q, todo.pop(0), held)
             for g, j in keys:
                 out_ref[g, j, side] = best[g, j]
             return 0
@@ -90,7 +93,7 @@
 
 def sent_kernel(level, flags_ref, t_ref, delay_ref, out_ref, wide, *scratch):
     def convert(q):
-        rows = pl.ds(pl.multiple_of(q * 2 * LANE, LANE), 2 * LANE)
+        rows = pl.ds(q * 2 * LANE, 2 * LANE)
         for j in range(8):
             value = delay_ref[level, rows, j * LANE : (j + 1) * LANE].astype(jnp.float32)
             wide[j, rows, :] = jnp.where(flags_ref[j // 4] > 0, value, jnp.float32(EMPTY))

time: 268 us -> 235 us (0.88)
  Pallas kernels: 78.2 us -> 45.5 us
    pallas_call x8, Pallas kernels: 78.2 us -> 45.5 us  [half_max(): pl.pallas_call(functools.partial(sent_kernel, level) if sent else kept_ke...]
  transfers between devices with their start and end apart: 5 -> 5, of which waited for: 1 -> 1; matrix products, arithmetic and copies ran while one was open for 0% -> 0% of each run, Pallas kernels for 15% -> 10%
where the time goes in v4:
time: 235 us; the launch traced here: 232 us
  blocking collectives  159 us (68%)
  Pallas kernels  45.5 us (19%)
  starting transfers between devices  16.1 us (7%)
  waiting for transfers between devices  5.94 us (3%)
  local copies, waits for them, and re-layouts  4.49 us (2%)
    all_to_all x11, blocking collectives, exchange(): return lax.all_to_all(value, axes, split_axis=0, concat_axis=0, tiled=True)  159 us
    pallas_call x8, Pallas kernels, half_max(): pl.pallas_call(functools.partial(sent_kernel, level) if sent else kept_ke...  45.5 us
    ppermute x4, starting transfers between devices, shards(): got = lax.ppermute(sent, 'z', neighbour)  12.6 us
    all_to_all x1, waiting for transfers between devices, exchange(): return lax.all_to_all(value, axes, split_axis=0, concat_axis=0, tiled=True)  5.93 us
  transfers between devices with their start and end apart: 5, of which 1 were waited for; matrix products, arithmetic and copies ran while one was open for 0% of the time, Pallas kernels for 10%

profile of v4, /device:TPU:1, one launch (start us, length us, event | category | flops | bytes accessed | tf_op | source)
XLA Modules:
  0.0 232.4 jit_solution(3074376660139649299)
XLA Ops:
  3.3 5.7 %sent_half.4 = (f32[4,4,2,8,128]{4,3,2,1,0:T(8,128)S(1)}, f32[8,512,128]{2,1,0:T(8,128)S(1)}) custom-call(s32[4]{0:T(128)S(1)} %get-tuple-element.18.flags_ref, f32[8,4,8,128]{3,2,1,0:T(8,128)S(1)} %bitcast.101, bf16[1,512,1024]{2,1,0:T(8,128)(2,1)S(1)} %slice.62.delay_ref), custom_call_target="tpu_custom_call" | custom-call | flops 33554432 | bytes 1048576 | tf_op jit(solution)/shard_map/sent_half/pallas_call | solution.py:116
  9.0 4.4 %collective-permute-start = (f32[4,4,2,8,128]{4,3,2,1,0:T(8,128)S(1)}, f32[4,4,2,8,128]{4,3,2,1,0:T(8,128)S(1)}, u32[]{:S(2)}, u32[]{:S(2)}) collective-permute-start(f32[4,4,2,8,128]{4,3,2,1,0:T(8,128)S(1)} %get-tuple-element.11), channel_id=1, source_target_pairs={{0,2},{2,0},{4,6},{6,4},{8,10},{10,8},{12,14},{14,12},{16,18},{18,... | collective-permute-start | bytes 393224 | tf_op jit(solution)/shard_map/ppermute | solution.py:154
  13.4 5.6 %kept_half.4 = f32[4,4,2,8,128]{4,3,2,1,0:T(8,128)S(1)} custom-call(s32[4]{0:T(128)S(1)} %get-tuple-element.18.flags_ref, f32[8,4,8,128]{3,2,1,0:T(8,128)S(1)} %bitcast.102, f32[8,512,128]{2,1,0:T(8,128)S(1)} %get-tuple-element.10.wide), custom_call_target="tpu_custom_call" | custom-call | flops 33554432 | bytes 1048576 | tf_op jit(solution)/shard_map/kept_half/pallas_call | solution.py:116
  19.0 15.5 %all_to_all.60 = f32[32,1,8,128]{3,2,1,0:T(8,128)S(1)} all-to-all(f32[32,1,8,128]{3,2,1,0:T(8,128)S(1)} %bitcast.104), channel_id=1, replica_groups=mesh['x'=4,'y'=4,'z'=16,'k'=2] {'x','y','k'}, dimensions={0} | all-to-all | bytes 262144 | tf_op jit(solution)/shard_map/all_to_all | solution.py:133
  34.6 25.4 %all_to_all.61 = f32[16,1,8,128]{3,2,1,0:T(8,128)S(1)} all-to-all(f32[16,1,8,128]{3,2,1,0:T(8,128)S(1)} %fusion.8), channel_id=1, replica_groups=mesh['x'=4,'y'=4,'z'=16,'k'=2] {'z'}, dimensions={0} | all-to-all | bytes 131072 | tf_op jit(solution)/shard_map/all_to_all | solution.py:133
  60.0 9.4 %all_to_all.62 = f32[16,2,8,128]{3,2,1,0:T(8,128)S(1)} all-to-all(f32[16,2,8,128]{3,2,1,0:T(8,128)S(1)} %broadcast_in_dim.27), channel_id=1, replica_groups=mesh['x'=4,'y'=4,'z'=16,'k'=2] {'x','y'}, dimensions={0} | all-to-all | bytes 262144 | tf_op jit(solution)/shard_map/all_to_all | solution.py:133
  69.4 5.7 %sent_half.5 = (f32[4,4,2,8,128]{4,3,2,1,0:T(8,128)S(1)}, f32[8,512,128]{2,1,0:T(8,128)S(1)}) custom-call(s32[4]{0:T(128)S(1)} %get-tuple-element.19.flags_ref, f32[4,4,2,8,128]{4,3,2,1,0:T(8,128)S(1)} %bitcast.97, bf16[4,512,1024]{2,1,0:T(8,128)(2,1)S(1)} %copy-done.1), custom_call_target="tpu_custom_call" | custom-call | flops 33554432 | bytes 1048576 | tf_op jit(solution)/shard_map/sent_half/pallas_call | solution.py:116
  75.2 2.7 %collective-permute-start.1 = (f32[4,4,2,8,128]{4,3,2,1,0:T(8,128)S(1)}, f32[4,4,2,8,128]{4,3,2,1,0:T(8,128)S(1)}, u32[]{:S(2)}, u32[]{:S(2)}) collective-permute-start(f32[4,4,2,8,128]{4,3,2,1,0:T(8,128)S(1)} %get-tuple-element.13), channel_id=1, source_target_pairs={{0,2},{2,0},{4,6},{6,4},{8,10},{10,8},{12,14},{14,12},{16,18},{18,... | collective-permute-start | bytes 393224 | tf_op jit(solution)/shard_map/ppermute | solution.py:154
  77.9 5.6 %kept_half.5 = f32[4,4,2,8,128]{4,3,2,1,0:T(8,128)S(1)} custom-call(s32[4]{0:T(128)S(1)} %get-tuple-element.19.flags_ref, f32[4,4,2,8,128]{4,3,2,1,0:T(8,128)S(1)} %bitcast.98, f32[8,512,128]{2,1,0:T(8,128)S(1)} %get-tuple-element.12.wide), custom_call_target="tpu_custom_call" | custom-call | flops 33554432 | bytes 1048576 | tf_op jit(solution)/shard_map/kept_half/pallas_call | solution.py:116
  83.6 14.8 %all_to_all.63 = f32[32,1,8,128]{3,2,1,0:T(8,128)S(1)} all-to-all(f32[32,1,8,128]{3,2,1,0:T(8,128)S(1)} %bitcast.105), channel_id=1, replica_groups=mesh['x'=4,'y'=4,'z'=16,'k'=2] {'x','y','k'}, dimensions={0} | all-to-all | bytes 262144 | tf_op jit(solution)/shard_map/all_to_all | solution.py:133
  98.4 14.5 %all_to_all.64 = f32[16,1,8,128]{3,2,1,0:T(8,128)S(1)} all-to-all(f32[16,1,8,128]{3,2,1,0:T(8,128)S(1)} %fusion.6), channel_id=1, replica_groups=mesh['x'=4,'y'=4,'z'=16,'k'=2] {'z'}, dimensions={0} | all-to-all | bytes 131072 | tf_op jit(solution)/shard_map/all_to_all | solution.py:133
  113.0 9.4 %all_to_all.65 = f32[16,2,8,128]{3,2,1,0:T(8,128)S(1)} all-to-all(f32[16,2,8,128]{3,2,1,0:T(8,128)S(1)} %broadcast_in_dim.28), channel_id=1, replica_groups=mesh['x'=4,'y'=4,'z'=16,'k'=2] {'x','y'}, dimensions={0} | all-to-all | bytes 262144 | tf_op jit(solution)/shard_map/all_to_all | solution.py:133
  122.4 5.7 %sent_half.6 = (f32[4,4,2,8,128]{4,3,2,1,0:T(8,128)S(1)}, f32[8,512,128]{2,1,0:T(8,128)S(1)}) custom-call(s32[4]{0:T(128)S(1)} %get-tuple-element.20.flags_ref, f32[4,4,2,8,128]{4,3,2,1,0:T(8,128)S(1)} %bitcast.99, bf16[4,512,1024]{2,1,0:T(8,128)(2,1)S(1)} %copy-done.1), custom_call_target="tpu_custom_call" | custom-call | flops 33554432 | bytes 1048576 | tf_op jit(solution)/shard_map/sent_half/pallas_call | solution.py:116
  130.9 5.6 %kept_half.6 = f32[4,4,2,8,128]{4,3,2,1,0:T(8,128)S(1)} custom-call(s32[4]{0:T(128)S(1)} %get-tuple-element.20.flags_ref, f32[4,4,2,8,128]{4,3,2,1,0:T(8,128)S(1)} %bitcast.100, f32[8,512,128]{2,1,0:T(8,128)S(1)} %get-tuple-element.14.wide), custom_call_target="tpu_custom_call" | custom-call | flops 33554432 | bytes 1048576 | tf_op jit(solution)/shard_map/kept_half/pallas_call | solution.py:116
  136.5 14.8 %all_to_all.66 = f32[32,1,8,128]{3,2,1,0:T(8,128)S(1)} all-to-all(f32[32,1,8,128]{3,2,1,0:T(8,128)S(1)} %bitcast.106), channel_id=1, replica_groups=mesh['x'=4,'y'=4,'z'=16,'k'=2] {'x','y','k'}, dimensions={0} | all-to-all | bytes 262144 | tf_op jit(solution)/shard_map/all_to_all | solution.py:133
  151.3 14.5 %all_to_all.67 = f32[16,1,8,128]{3,2,1,0:T(8,128)S(1)} all-to-all(f32[16,1,8,128]{3,2,1,0:T(8,128)S(1)} %fusion.4), channel_id=1, replica_groups=mesh['x'=4,'y'=4,'z'=16,'k'=2] {'z'}, dimensions={0} | all-to-all | bytes 131072 | tf_op jit(solution)/shard_map/all_to_all | solution.py:133
  165.9 9.4 %all_to_all.68 = f32[16,2,8,128]{3,2,1,0:T(8,128)S(1)} all-to-all(f32[16,2,8,128]{3,2,1,0:T(8,128)S(1)} %broadcast_in_dim.29), channel_id=1, replica_groups=mesh['x'=4,'y'=4,'z'=16,'k'=2] {'x','y'}, dimensions={0} | all-to-all | bytes 262144 | tf_op jit(solution)/shard_map/all_to_all | solution.py:133
  175.3 5.8 %sent_half.7 = (f32[4,4,2,8,128]{4,3,2,1,0:T(8,128)S(1)}, f32[8,512,128]{2,1,0:T(8,128)S(1)}) custom-call(s32[4]{0:T(128)S(1)} %get-tuple-element.21.flags_ref, f32[4,4,2,8,128]{4,3,2,1,0:T(8,128)S(1)} %bitcast.95, bf16[4,512,1024]{2,1,0:T(8,128)(2,1)S(1)} %copy-done.1), custom_call_target="tpu_custom_call" | custom-call | flops 33554432 | bytes 1048576 | tf_op jit(solution)/shard_map/sent_half/pallas_call | solution.py:116
  181.1 2.7 %collective-permute-start.3 = (f32[4,4,2,8,128]{4,3,2,1,0:T(8,128)S(1)}, f32[4,4,2,8,128]{4,3,2,1,0:T(8,128)S(1)}, u32[]{:S(2)}, u32[]{:S(2)}) collective-permute-start(f32[4,4,2,8,128]{4,3,2,1,0:T(8,128)S(1)} %get-tuple-element.17), channel_id=1, source_target_pairs={{0,2},{2,0},{4,6},{6,4},{8,10},{10,8},{12,14},{14,12},{16,18},{18,... | collective-permute-start | bytes 393224 | tf_op jit(solution)/shard_map/ppermute | solution.py:154
  183.8 5.6 %kept_half.7 = f32[4,4,2,8,128]{4,3,2,1,0:T(8,128)S(1)} custom-call(s32[4]{0:T(128)S(1)} %get-tuple-element.21.flags_ref, f32[4,4,2,8,128]{4,3,2,1,0:T(8,128)S(1)} %bitcast.96, f32[8,512,128]{2,1,0:T(8,128)S(1)} %get-tuple-element.16.wide), custom_call_target="tpu_custom_call" | custom-call | flops 33554432 | bytes 1048576 | tf_op jit(solution)/shard_map/kept_half/pallas_call | solution.py:116
  189.7 16.1 %all_to_all.69 = f32[32,2,8,128]{3,2,1,0:T(8,128)S(1)} all-to-all(f32[32,2,8,128]{3,2,1,0:T(8,128)S(1)} %pad_maximum_fusion), channel_id=1, replica_groups=mesh['x'=4,'y'=4,'z'=16,'k'=2] {'x','y','k'}, dimensions={0} | all-to-all | bytes 524288 | tf_op jit(solution)/shard_map/all_to_all | solution.py:133
  205.9 15.0 %all_to_all.70 = f32[16,2,8,128]{3,2,1,0:T(8,128)S(1)} all-to-all(f32[16,2,8,128]{3,2,1,0:T(8,128)S(1)} %pad_maximum_fusion.1), channel_id=1, replica_groups=mesh['x'=4,'y'=4,'z'=16,'k'=2] {'z'}, dimensions={0} | all-to-all | bytes 262144 | tf_op jit(solution)/shard_map/all_to_all | solution.py:133
  221.6 3.5 %all-to-all-start.11 = ((f32[16,2,8,128]{3,2,1,0:T(8,128)}), f32[16,2,8,128]{3,2,1,0:T(8,128)S(1)}, u32[]{:S(2)}, u32[]{:S(2)}) async-start(f32[16,2,8,128]{3,2,1,0:T(8,128)} %broadcast_in_dim.34), calls=%async_computation.11 | async-start | bytes 262144 | tf_op jit(solution)/shard_map/all_to_all | solution.py:133
  225.8 5.9 %all-to-all-done.11 = f32[16,2,8,128]{3,2,1,0:T(8,128)S(1)} async-done(((f32[16,2,8,128]{3,2,1,0:T(8,128)}), f32[16,2,8,128]{3,2,1,0:T(8,128)S(1)}, u32[]{:S(2)}, u32[]{:S(2)}) %all-to-all-start.11) | async-done | bytes 131104 | tf_op jit(solution)/shard_map/all_to_all | solution.py:133
  (47 shorter events, 7.8 us)
Async XLA Ops:
  0.6 0.8 copy-start
  0.6 2.6 %copy-start.2 = (f32[64,512]{1,0:T(8,128)S(1)}, f32[64,512]{1,0:T(8,128)}, u32[]{:S(2)}) copy-start(f32[64,512]{1,0:T(8,128)} %param.3) | copy-start | bytes 393220
  3.3 66.2 %copy-start.1 = (bf16[4,512,1024]{2,1,0:T(8,128)(2,1)S(1)}, bf16[4,512,1024]{2,1,0:T(8,128)(2,1)}, u32[]{:S(2)}) copy-start(bf16[4,512,1024]{2,1,0:T(8,128)(2,1)} %delay_ref.5) | copy-start | bytes 12582916
  9.0 10.0 %collective-permute-start = (f32[4,4,2,8,128]{4,3,2,1,0:T(8,128)S(1)}, f32[4,4,2,8,128]{4,3,2,1,0:T(8,128)S(1)}, u32[]{:S(2)}, u32[]{:S(2)}) collective-permute-start(f32[4,4,2,8,128]{4,3,2,1,0:T(8,128)S(1)} %get-tuple-element.11), channel_id=1, source_target_pairs={{0,2},{2,0},{4,6},{6,4},{8,10},{10,8},{12,14},{14,12},{16,18},{18,... | collective-permute-start | bytes 393224 | tf_op jit(solution)/shard_map/ppermute | solution.py:154
  75.2 8.4 %collective-permute-start.1 = (f32[4,4,2,8,128]{4,3,2,1,0:T(8,128)S(1)}, f32[4,4,2,8,128]{4,3,2,1,0:T(8,128)S(1)}, u32[]{:S(2)}, u32[]{:S(2)}) collective-permute-start(f32[4,4,2,8,128]{4,3,2,1,0:T(8,128)S(1)} %get-tuple-element.13), channel_id=1, source_target_pairs={{0,2},{2,0},{4,6},{6,4},{8,10},{10,8},{12,14},{14,12},{16,18},{18,... | collective-permute-start | bytes 393224 | tf_op jit(solution)/shard_map/ppermute | solution.py:154
  128.1 8.4 %collective-permute-start.2 = (f32[4,4,2,8,128]{4,3,2,1,0:T(8,128)S(1)}, f32[4,4,2,8,128]{4,3,2,1,0:T(8,128)S(1)}, u32[]{:S(2)}, u32[]{:S(2)}) collective-permute-start(f32[4,4,2,8,128]{4,3,2,1,0:T(8,128)S(1)} %get-tuple-element.15), channel_id=1, source_target_pairs={{0,2},{2,0},{4,6},{6,4},{8,10},{10,8},{12,14},{14,12},{16,18},{18,... | collective-permute-start | bytes 393224 | tf_op jit(solution)/shard_map/ppermute | solution.py:154
  181.1 8.4 %collective-permute-start.3 = (f32[4,4,2,8,128]{4,3,2,1,0:T(8,128)S(1)}, f32[4,4,2,8,128]{4,3,2,1,0:T(8,128)S(1)}, u32[]{:S(2)}, u32[]{:S(2)}) collective-permute-start(f32[4,4,2,8,128]{4,3,2,1,0:T(8,128)S(1)} %get-tuple-element.17), channel_id=1, source_target_pairs={{0,2},{2,0},{4,6},{6,4},{8,10},{10,8},{12,14},{14,12},{16,18},{18,... | collective-permute-start | bytes 393224 | tf_op jit(solution)/shard_map/ppermute | solution.py:154
  221.6 10.2 %all-to-all-start.11 = ((f32[16,2,8,128]{3,2,1,0:T(8,128)}), f32[16,2,8,128]{3,2,1,0:T(8,128)S(1)}, u32[]{:S(2)}, u32[]{:S(2)}) async-start(f32[16,2,8,128]{3,2,1,0:T(8,128)} %broadcast_in_dim.34), calls=%async_computation.11 | async-start | bytes 262144 | tf_op jit(solution)/shard_map/all_to_all | solution.py:133

commit v5 on v4

--- a/solution.py
+++ b/solution.py
@@ -11,6 +11,7 @@
 
 SUB, LANE = 8, 128
 EMPTY = -1000000000.0
+BOUND = 1000000000.0
 HALF = 4
 TILES = 4
 SHIFT = 8
@@ -91,21 +92,27 @@
     return lambda g, tile: t_ref[g, tile, half]
 
 
-def sent_kernel(level, flags_ref, t_ref, delay_ref, out_ref, wide, *scratch):
+def parity():
+    return lax.rem(lax.axis_index("z"), 2)
+
+
+def sent_kernel(level, caps_ref, t_ref, delay_ref, out_ref, wide, *scratch):
+    slab = level if delay_ref.shape[0] > 1 else 0
+
     def convert(q):
         rows = pl.ds(q * 2 * LANE, 2 * LANE)
         for j in range(8):
-            value = delay_ref[level, rows, j * LANE : (j + 1) * LANE].astype(jnp.float32)
-            wide[j, rows, :] = jnp.where(flags_ref[j // 4] > 0, value, jnp.float32(EMPTY))
+            value = delay_ref[slab, rows, j * LANE : (j + 1) * LANE].astype(jnp.float32)
+            wide[j, rows, :] = jnp.minimum(value, caps_ref[level, j // 4, 0:1, :])
 
-    half_body(times_of(t_ref, flags_ref[2]), convert, wide, out_ref, *scratch)
+    half_body(times_of(t_ref, 1 - parity()), convert, wide, out_ref, *scratch)
 
 
-def kept_kernel(flags_ref, t_ref, wide, out_ref, *scratch):
-    half_body(times_of(t_ref, flags_ref[3]), lambda q: None, wide, out_ref, *scratch)
+def kept_kernel(t_ref, wide, out_ref, *scratch):
+    half_body(times_of(t_ref, parity()), lambda q: None, wide, out_ref, *scratch)
 
 
-def half_max(level, flags, times, source, shape):
+def half_max(level, caps, times, source, shape):
     levels, rows, width = shape
     work = HALF * SUB * rows * width
     vmem = pl.BlockSpec(memory_space=pltpu.VMEM)
@@ -116,7 +123,7 @@
     return pl.pallas_call(
         functools.partial(sent_kernel, level) if sent else kept_kernel,
         out_shape=(out, wide) if sent else out,
-        in_specs=[pl.BlockSpec(memory_space=pltpu.SMEM), vmem, vmem],
+        in_specs=[vmem] * (3 if sent else 2),
         out_specs=(vmem, vmem) if sent else vmem,
         scratch_shapes=[
             spread,
@@ -126,7 +133,7 @@
         compiler_params=pltpu.CompilerParams(vmem_limit_bytes=16 * 1024 * 1024),
         cost_estimate=pl.CostEstimate(flops=2 * work, bytes_accessed=2 * rows * width, transcendentals=0),
         name="sent_half" if sent else "kept_half",
-    )(flags, times, source)
+    )(*((caps, times, source) if sent else (times, source)))
 
 
 def exchange(value, axes):
@@ -142,17 +149,17 @@
     odd = lax.axis_index("z") % 2
     col = lax.axis_index("z") * lax.axis_size("k") + lax.axis_index("k")
     flags = lax.dynamic_slice(occupancy, (0, col, place * 2), (levels, 1, 2))[:, 0, :]
-    halves = jnp.broadcast_to(jnp.stack([1 - odd, odd])[None], (levels, 2))
-    flags = jnp.concatenate([flags, halves], axis=1)
+    caps = jnp.where(flags > 0, jnp.float32(BOUND), jnp.float32(EMPTY))
+    caps = jnp.broadcast_to(caps[:, :, None, None], (levels, 2, SUB, LANE))
     groups, tiles = scenarios // SUB, pins // LANE
     neighbour = [(z, z ^ 1) for z in range(depth)]
     times = jnp.transpose(arrival.reshape(groups, SUB, tiles, LANE), (0, 2, 1, 3))
     worst = None
     for level in range(levels):
         last = level == levels - 1
-        sent, wide = half_max(0 if level == 0 else level, flags[level], times, delay[:1] if level == 0 else delay, delay.shape)
+        sent, wide = half_max(level, caps, times, delay[:1] if level == 0 else delay, delay.shape)
         got = lax.ppermute(sent, "z", neighbour)
-        kept = half_max(None, flags[level], times, wide, delay.shape)
+        kept = half_max(None, None, times, wide, delay.shape)
         best = jnp.maximum(kept, got)
         parts = best.reshape(plane * 2, 1, SUB, LANE)
         if last:

time: 235 us -> 231 us (0.983)
  Pallas kernels: 45.5 us -> 41.2 us
    pallas_call x8, Pallas kernels: 45.5 us -> 41.2 us  [half_max(): pl.pallas_call(functools.partial(sent_kernel, level) if sent else kept_ke...]
  transfers between devices with their start and end apart: 5 -> 5, of which waited for: 1 -> 1; matrix products, arithmetic and copies ran while one was open for 0% -> 0% of each run, Pallas kernels for 10% -> 9%
where the time goes in v5:
time: 231 us; the launch traced here: 228 us
  blocking collectives  159 us (69%)
  Pallas kernels  41.2 us (18%)
  starting transfers between devices  16.1 us (7%)
  waiting for transfers between devices  5.94 us (3%)
  local copies, waits for them, and re-layouts  3.47 us (2%)
    all_to_all x11, blocking collectives, exchange(): return lax.all_to_all(value, axes, split_axis=0, concat_axis=0, tiled=True)  159 us
    pallas_call x8, Pallas kernels, half_max(): pl.pallas_call(functools.partial(sent_kernel, level) if sent else kept_ke...  41.2 us
    ppermute x4, starting transfers between devices, shards(): got = lax.ppermute(sent, 'z', neighbour)  12.6 us
    all_to_all x1, waiting for transfers between devices, exchange(): return lax.all_to_all(value, axes, split_axis=0, concat_axis=0, tiled=True)  5.93 us
  transfers between devices with their start and end apart: 5, of which 1 were waited for; matrix products, arithmetic and copies ran while one was open for 0% of the time, Pallas kernels for 9%

profile of v5, /device:TPU:1, one launch (start us, length us, event | category | flops | bytes accessed | tf_op | source)
XLA Modules:
  0.0 227.7 jit_solution(5422033330884174713)
XLA Ops:
  2.9 5.2 %sent_half.4 = (f32[4,4,2,8,128]{4,3,2,1,0:T(8,128)S(1)}, f32[8,512,128]{2,1,0:T(8,128)S(1)}) custom-call(f32[4,2,8,128]{3,2,1,0:T(8,128)S(1)} %broadcast_in_dim.36.caps_ref, f32[8,4,8,128]{3,2,1,0:T(8,128)S(1)} %bitcast.99, bf16[1,512,1024]{2,1,0:T(8,128)(2,1)S(1)} %slice.42.delay_ref), custom_call_target="tpu_custom_call" | custom-call | flops 33554432 | bytes 1048576 | tf_op jit(solution)/shard_map/sent_half/pallas_call | solution.py:123
  8.1 4.4 %collective-permute-start = (f32[4,4,2,8,128]{4,3,2,1,0:T(8,128)S(1)}, f32[4,4,2,8,128]{4,3,2,1,0:T(8,128)S(1)}, u32[]{:S(2)}, u32[]{:S(2)}) collective-permute-start(f32[4,4,2,8,128]{4,3,2,1,0:T(8,128)S(1)} %get-tuple-element.11), channel_id=1, source_target_pairs={{0,2},{2,0},{4,6},{6,4},{8,10},{10,8},{12,14},{14,12},{16,18},{18,... | collective-permute-start | bytes 393224 | tf_op jit(solution)/shard_map/ppermute | solution.py:161
  12.5 5.1 %kept_half.4 = f32[4,4,2,8,128]{4,3,2,1,0:T(8,128)S(1)} custom-call(f32[8,4,8,128]{3,2,1,0:T(8,128)S(1)} %bitcast.100, f32[8,512,128]{2,1,0:T(8,128)S(1)} %get-tuple-element.10.wide), custom_call_target="tpu_custom_call" | custom-call | flops 33554432 | bytes 1048576 | tf_op jit(solution)/shard_map/kept_half/pallas_call | solution.py:123
  17.6 15.5 %all_to_all.60 = f32[32,1,8,128]{3,2,1,0:T(8,128)S(1)} all-to-all(f32[32,1,8,128]{3,2,1,0:T(8,128)S(1)} %bitcast.102), channel_id=1, replica_groups=mesh['x'=4,'y'=4,'z'=16,'k'=2] {'x','y','k'}, dimensions={0} | all-to-all | bytes 262144 | tf_op jit(solution)/shard_map/all_to_all | solution.py:140
  33.1 25.4 %all_to_all.61 = f32[16,1,8,128]{3,2,1,0:T(8,128)S(1)} all-to-all(f32[16,1,8,128]{3,2,1,0:T(8,128)S(1)} %fusion.8), channel_id=1, replica_groups=mesh['x'=4,'y'=4,'z'=16,'k'=2] {'z'}, dimensions={0} | all-to-all | bytes 131072 | tf_op jit(solution)/shard_map/all_to_all | solution.py:140
  58.6 9.4 %all_to_all.62 = f32[16,2,8,128]{3,2,1,0:T(8,128)S(1)} all-to-all(f32[16,2,8,128]{3,2,1,0:T(8,128)S(1)} %broadcast_in_dim.37), channel_id=1, replica_groups=mesh['x'=4,'y'=4,'z'=16,'k'=2] {'x','y'}, dimensions={0} | all-to-all | bytes 262144 | tf_op jit(solution)/shard_map/all_to_all | solution.py:140
  68.0 5.2 %sent_half.5 = (f32[4,4,2,8,128]{4,3,2,1,0:T(8,128)S(1)}, f32[8,512,128]{2,1,0:T(8,128)S(1)}) custom-call(f32[4,2,8,128]{3,2,1,0:T(8,128)S(1)} %broadcast_in_dim.36.caps_ref, f32[4,4,2,8,128]{4,3,2,1,0:T(8,128)S(1)} %bitcast.95, bf16[4,512,1024]{2,1,0:T(8,128)(2,1)S(1)} %copy-done), custom_call_target="tpu_custom_call" | custom-call | flops 33554432 | bytes 1048576 | tf_op jit(solution)/shard_map/sent_half/pallas_call | solution.py:123
  73.2 2.7 %collective-permute-start.1 = (f32[4,4,2,8,128]{4,3,2,1,0:T(8,128)S(1)}, f32[4,4,2,8,128]{4,3,2,1,0:T(8,128)S(1)}, u32[]{:S(2)}, u32[]{:S(2)}) collective-permute-start(f32[4,4,2,8,128]{4,3,2,1,0:T(8,128)S(1)} %get-tuple-element.13), channel_id=1, source_target_pairs={{0,2},{2,0},{4,6},{6,4},{8,10},{10,8},{12,14},{14,12},{16,18},{18,... | collective-permute-start | bytes 393224 | tf_op jit(solution)/shard_map/ppermute | solution.py:161
  75.9 5.1 %kept_half.5 = f32[4,4,2,8,128]{4,3,2,1,0:T(8,128)S(1)} custom-call(f32[4,4,2,8,128]{4,3,2,1,0:T(8,128)S(1)} %bitcast.96, f32[8,512,128]{2,1,0:T(8,128)S(1)} %get-tuple-element.12.wide), custom_call_target="tpu_custom_call" | custom-call | flops 33554432 | bytes 1048576 | tf_op jit(solution)/shard_map/kept_half/pallas_call | solution.py:123
  81.1 14.8 %all_to_all.63 = f32[32,1,8,128]{3,2,1,0:T(8,128)S(1)} all-to-all(f32[32,1,8,128]{3,2,1,0:T(8,128)S(1)} %bitcast.103), channel_id=1, replica_groups=mesh['x'=4,'y'=4,'z'=16,'k'=2] {'x','y','k'}, dimensions={0} | all-to-all | bytes 262144 | tf_op jit(solution)/shard_map/all_to_all | solution.py:140
  95.9 14.5 %all_to_all.64 = f32[16,1,8,128]{3,2,1,0:T(8,128)S(1)} all-to-all(f32[16,1,8,128]{3,2,1,0:T(8,128)S(1)} %fusion.6), channel_id=1, replica_groups=mesh['x'=4,'y'=4,'z'=16,'k'=2] {'z'}, dimensions={0} | all-to-all | bytes 131072 | tf_op jit(solution)/shard_map/all_to_all | solution.py:140
  110.4 9.4 %all_to_all.65 = f32[16,2,8,128]{3,2,1,0:T(8,128)S(1)} all-to-all(f32[16,2,8,128]{3,2,1,0:T(8,128)S(1)} %broadcast_in_dim.38), channel_id=1, replica_groups=mesh['x'=4,'y'=4,'z'=16,'k'=2] {'x','y'}, dimensions={0} | all-to-all | bytes 262144 | tf_op jit(solution)/shard_map/all_to_all | solution.py:140
  119.8 5.2 %sent_half.6 = (f32[4,4,2,8,128]{4,3,2,1,0:T(8,128)S(1)}, f32[8,512,128]{2,1,0:T(8,128)S(1)}) custom-call(f32[4,2,8,128]{3,2,1,0:T(8,128)S(1)} %broadcast_in_dim.36.caps_ref, f32[4,4,2,8,128]{4,3,2,1,0:T(8,128)S(1)} %bitcast.97, bf16[4,512,1024]{2,1,0:T(8,128)(2,1)S(1)} %copy-done), custom_call_target="tpu_custom_call" | custom-call | flops 33554432 | bytes 1048576 | tf_op jit(solution)/shard_map/sent_half/pallas_call | solution.py:123
  125.1 2.7 %collective-permute-start.2 = (f32[4,4,2,8,128]{4,3,2,1,0:T(8,128)S(1)}, f32[4,4,2,8,128]{4,3,2,1,0:T(8,128)S(1)}, u32[]{:S(2)}, u32[]{:S(2)}) collective-permute-start(f32[4,4,2,8,128]{4,3,2,1,0:T(8,128)S(1)} %get-tuple-element.15), channel_id=1, source_target_pairs={{0,2},{2,0},{4,6},{6,4},{8,10},{10,8},{12,14},{14,12},{16,18},{18,... | collective-permute-start | bytes 393224 | tf_op jit(solution)/shard_map/ppermute | solution.py:161
  127.8 5.1 %kept_half.6 = f32[4,4,2,8,128]{4,3,2,1,0:T(8,128)S(1)} custom-call(f32[4,4,2,8,128]{4,3,2,1,0:T(8,128)S(1)} %bitcast.98, f32[8,512,128]{2,1,0:T(8,128)S(1)} %get-tuple-element.14.wide), custom_call_target="tpu_custom_call" | custom-call | flops 33554432 | bytes 1048576 | tf_op jit(solution)/shard_map/kept_half/pallas_call | solution.py:123
  132.9 14.8 %all_to_all.66 = f32[32,1,8,128]{3,2,1,0:T(8,128)S(1)} all-to-all(f32[32,1,8,128]{3,2,1,0:T(8,128)S(1)} %bitcast.104), channel_id=1, replica_groups=mesh['x'=4,'y'=4,'z'=16,'k'=2] {'x','y','k'}, dimensions={0} | all-to-all | bytes 262144 | tf_op jit(solution)/shard_map/all_to_all | solution.py:140
  147.8 14.5 %all_to_all.67 = f32[16,1,8,128]{3,2,1,0:T(8,128)S(1)} all-to-all(f32[16,1,8,128]{3,2,1,0:T(8,128)S(1)} %fusion.4), channel_id=1, replica_groups=mesh['x'=4,'y'=4,'z'=16,'k'=2] {'z'}, dimensions={0} | all-to-all | bytes 131072 | tf_op jit(solution)/shard_map/all_to_all | solution.py:140
  162.3 9.4 %all_to_all.68 = f32[16,2,8,128]{3,2,1,0:T(8,128)S(1)} all-to-all(f32[16,2,8,128]{3,2,1,0:T(8,128)S(1)} %broadcast_in_dim.39), channel_id=1, replica_groups=mesh['x'=4,'y'=4,'z'=16,'k'=2] {'x','y'}, dimensions={0} | all-to-all | bytes 262144 | tf_op jit(solution)/shard_map/all_to_all | solution.py:140
  171.7 5.2 %sent_half.7 = (f32[4,4,2,8,128]{4,3,2,1,0:T(8,128)S(1)}, f32[8,512,128]{2,1,0:T(8,128)S(1)}) custom-call(f32[4,2,8,128]{3,2,1,0:T(8,128)S(1)} %broadcast_in_dim.36.caps_ref, f32[4,4,2,8,128]{4,3,2,1,0:T(8,128)S(1)} %bitcast.93, bf16[4,512,1024]{2,1,0:T(8,128)(2,1)S(1)} %copy-done), custom_call_target="tpu_custom_call" | custom-call | flops 33554432 | bytes 1048576 | tf_op jit(solution)/shard_map/sent_half/pallas_call | solution.py:123
  179.7 5.1 %kept_half.7 = f32[4,4,2,8,128]{4,3,2,1,0:T(8,128)S(1)} custom-call(f32[4,4,2,8,128]{4,3,2,1,0:T(8,128)S(1)} %bitcast.94, f32[8,512,128]{2,1,0:T(8,128)S(1)} %get-tuple-element.16.wide), custom_call_target="tpu_custom_call" | custom-call | flops 33554432 | bytes 1048576 | tf_op jit(solution)/shard_map/kept_half/pallas_call | solution.py:123
  185.0 16.1 %all_to_all.69 = f32[32,2,8,128]{3,2,1,0:T(8,128)S(1)} all-to-all(f32[32,2,8,128]{3,2,1,0:T(8,128)S(1)} %pad_maximum_fusion), channel_id=1, replica_groups=mesh['x'=4,'y'=4,'z'=16,'k'=2] {'x','y','k'}, dimensions={0} | all-to-all | bytes 524288 | tf_op jit(solution)/shard_map/all_to_all | solution.py:140
  201.2 15.0 %all_to_all.70 = f32[16,2,8,128]{3,2,1,0:T(8,128)S(1)} all-to-all(f32[16,2,8,128]{3,2,1,0:T(8,128)S(1)} %pad_maximum_fusion.1), channel_id=1, replica_groups=mesh['x'=4,'y'=4,'z'=16,'k'=2] {'z'}, dimensions={0} | all-to-all | bytes 262144 | tf_op jit(solution)/shard_map/all_to_all | solution.py:140
  216.9 3.5 %all-to-all-start.11 = ((f32[16,2,8,128]{3,2,1,0:T(8,128)}), f32[16,2,8,128]{3,2,1,0:T(8,128)S(1)}, u32[]{:S(2)}, u32[]{:S(2)}) async-start(f32[16,2,8,128]{3,2,1,0:T(8,128)} %broadcast_in_dim.73), calls=%async_computation.11 | async-start | bytes 262144 | tf_op jit(solution)/shard_map/all_to_all | solution.py:140
  221.1 5.9 %all-to-all-done.11 = f32[16,2,8,128]{3,2,1,0:T(8,128)S(1)} async-done(((f32[16,2,8,128]{3,2,1,0:T(8,128)}), f32[16,2,8,128]{3,2,1,0:T(8,128)S(1)}, u32[]{:S(2)}, u32[]{:S(2)}) %all-to-all-start.11) | async-done | bytes 131104 | tf_op jit(solution)/shard_map/all_to_all | solution.py:140
  (41 shorter events, 7.4 us)
Async XLA Ops:
  0.6 2.2 copy-start.1
  2.9 65.1 %copy-start = (bf16[4,512,1024]{2,1,0:T(8,128)(2,1)S(1)}, bf16[4,512,1024]{2,1,0:T(8,128)(2,1)}, u32[]{:S(2)}) copy-start(bf16[4,512,1024]{2,1,0:T(8,128)(2,1)} %delay_ref.5) | copy-start | bytes 12582916
  8.1 9.5 %collective-permute-start = (f32[4,4,2,8,128]{4,3,2,1,0:T(8,128)S(1)}, f32[4,4,2,8,128]{4,3,2,1,0:T(8,128)S(1)}, u32[]{:S(2)}, u32[]{:S(2)}) collective-permute-start(f32[4,4,2,8,128]{4,3,2,1,0:T(8,128)S(1)} %get-tuple-element.11), channel_id=1, source_target_pairs={{0,2},{2,0},{4,6},{6,4},{8,10},{10,8},{12,14},{14,12},{16,18},{18,... | collective-permute-start | bytes 393224 | tf_op jit(solution)/shard_map/ppermute | solution.py:161
  73.2 7.9 %collective-permute-start.1 = (f32[4,4,2,8,128]{4,3,2,1,0:T(8,128)S(1)}, f32[4,4,2,8,128]{4,3,2,1,0:T(8,128)S(1)}, u32[]{:S(2)}, u32[]{:S(2)}) collective-permute-start(f32[4,4,2,8,128]{4,3,2,1,0:T(8,128)S(1)} %get-tuple-element.13), channel_id=1, source_target_pairs={{0,2},{2,0},{4,6},{6,4},{8,10},{10,8},{12,14},{14,12},{16,18},{18,... | collective-permute-start | bytes 393224 | tf_op jit(solution)/shard_map/ppermute | solution.py:161
  125.1 7.9 %collective-permute-start.2 = (f32[4,4,2,8,128]{4,3,2,1,0:T(8,128)S(1)}, f32[4,4,2,8,128]{4,3,2,1,0:T(8,128)S(1)}, u32[]{:S(2)}, u32[]{:S(2)}) collective-permute-start(f32[4,4,2,8,128]{4,3,2,1,0:T(8,128)S(1)} %get-tuple-element.15), channel_id=1, source_target_pairs={{0,2},{2,0},{4,6},{6,4},{8,10},{10,8},{12,14},{14,12},{16,18},{18,... | collective-permute-start | bytes 393224 | tf_op jit(solution)/shard_map/ppermute | solution.py:161
  176.9 7.9 %collective-permute-start.3 = (f32[4,4,2,8,128]{4,3,2,1,0:T(8,128)S(1)}, f32[4,4,2,8,128]{4,3,2,1,0:T(8,128)S(1)}, u32[]{:S(2)}, u32[]{:S(2)}) collective-permute-start(f32[4,4,2,8,128]{4,3,2,1,0:T(8,128)S(1)} %get-tuple-element.17), channel_id=1, source_target_pairs={{0,2},{2,0},{4,6},{6,4},{8,10},{10,8},{12,14},{14,12},{16,18},{18,... | collective-permute-start | bytes 393224 | tf_op jit(solution)/shard_map/ppermute | solution.py:161
  216.9 10.2 %all-to-all-start.11 = ((f32[16,2,8,128]{3,2,1,0:T(8,128)}), f32[16,2,8,128]{3,2,1,0:T(8,128)S(1)}, u32[]{:S(2)}, u32[]{:S(2)}) async-start(f32[16,2,8,128]{3,2,1,0:T(8,128)} %broadcast_in_dim.73), calls=%async_computation.11 | async-start | bytes 262144 | tf_op jit(solution)/shard_map/all_to_all | solution.py:140

commit v6 on v5

--- a/solution.py
+++ b/solution.py
@@ -165,6 +165,7 @@
         if last:
             top = jnp.max(jnp.max(best, axis=(1, 2)), axis=2)
             spot = lax.broadcasted_iota(jnp.int32, (HALF, SUB, LANE), 0) + odd * HALF
+            spot = spot * SUB + lax.broadcasted_iota(jnp.int32, (HALF, SUB, LANE), 1)
             here = lax.broadcasted_iota(jnp.int32, (HALF, SUB, LANE), 2) == spot
             top = jnp.max(jnp.where(here, top[:, :, None], EMPTY), axis=0)
             parts = jnp.concatenate([parts, jnp.broadcast_to(top[None, None], parts.shape)], axis=1)
@@ -176,8 +177,10 @@
             got = jnp.concatenate([got[:, :1], jnp.broadcast_to(top[None, None], (plane, 1, SUB, LANE))], axis=1)
         got = exchange(got, "z")
         if last:
-            worst = jnp.transpose(jnp.max(got[:, 1], axis=0)[:, :groups]).reshape(scenarios)
+            worst = jnp.max(got[:, 1], axis=(0, 1))[:scenarios]
         got = jnp.max(got[:, 0].reshape(depth // 2, 2, SUB, LANE), axis=0)
+        if last:
+            got, worst = lax.optimization_barrier((got, worst))
         whole = exchange(jnp.broadcast_to(got[None], (plane, 2, SUB, LANE)), ("x", "y"))
         times = whole.reshape(HALF, tiles, 2, SUB, LANE)
     final = jnp.transpose(times, (2, 0, 3, 1, 4)).reshape(scenarios, pins)

time: 231 us -> 230 us (level)
  blocking collectives: 159 us -> 168 us
  waiting for transfers between devices: 5.94 us -> 0.01 us
  starting transfers between devices: 16.1 us -> 12.6 us
    all_to_all x11 -> x12, blocking collectives: 159 us -> 168 us  [exchange(): return lax.all_to_all(value, axes, split_axis=0, concat_axis=0, tiled=True)]
    all_to_all x1 -> x0, waiting for transfers between devices: 5.93 us -> none  [exchange(): return lax.all_to_all(value, axes, split_axis=0, concat_axis=0, tiled=True)]
    all_to_all x1 -> x0, starting transfers between devices: 3.51 us -> none  [exchange(): return lax.all_to_all(value, axes, split_axis=0, concat_axis=0, tiled=True)]
  transfers between devices with their start and end apart: 5 -> 4, of which waited for: 1 -> 0; matrix products, arithmetic and copies ran while one was open for 0% -> 0% of each run, Pallas kernels for 9% -> 9%
where the time goes in v6:
time: 230 us; the launch traced here: 227 us
  blocking collectives  168 us (73%)
  Pallas kernels  41.2 us (18%)
  starting transfers between devices  12.6 us (5%)
    all_to_all x12, blocking collectives, exchange(): return lax.all_to_all(value, axes, split_axis=0, concat_axis=0, tiled=True)  168 us
    pallas_call x8, Pallas kernels, half_max(): pl.pallas_call(functools.partial(sent_kernel, level) if sent else kept_ke...  41.2 us
    ppermute x4, starting transfers between devices, shards(): got = lax.ppermute(sent, 'z', neighbour)  12.6 us
  transfers between devices with their start and end apart: 4, of which 0 were waited for; matrix products, arithmetic and copies ran while one was open for 0% of the time, Pallas kernels for 9%

profile of v6, /device:TPU:1, one launch (start us, length us, event | category | flops | bytes accessed | tf_op | source)
XLA Modules:
  0.0 226.9 jit_solution(7417008796980440935)
XLA Ops:
  2.9 5.2 %sent_half.4 = (f32[4,4,2,8,128]{4,3,2,1,0:T(8,128)S(1)}, f32[8,512,128]{2,1,0:T(8,128)S(1)}) custom-call(f32[4,2,8,128]{3,2,1,0:T(8,128)S(1)} %broadcast_in_dim.36.caps_ref, f32[8,4,8,128]{3,2,1,0:T(8,128)S(1)} %bitcast.94, bf16[1,512,1024]{2,1,0:T(8,128)(2,1)S(1)} %slice.42.delay_ref), custom_call_target="tpu_custom_call" | custom-call | flops 33554432 | bytes 1048576 | tf_op jit(solution)/shard_map/sent_half/pallas_call | solution.py:123
  8.1 4.4 %collective-permute-start = (f32[4,4,2,8,128]{4,3,2,1,0:T(8,128)S(1)}, f32[4,4,2,8,128]{4,3,2,1,0:T(8,128)S(1)}, u32[]{:S(2)}, u32[]{:S(2)}) collective-permute-start(f32[4,4,2,8,128]{4,3,2,1,0:T(8,128)S(1)} %get-tuple-element.13), channel_id=1, source_target_pairs={{0,2},{2,0},{4,6},{6,4},{8,10},{10,8},{12,14},{14,12},{16,18},{18,... | collective-permute-start | bytes 393224 | tf_op jit(solution)/shard_map/ppermute | solution.py:161
  12.5 5.1 %kept_half.4 = f32[4,4,2,8,128]{4,3,2,1,0:T(8,128)S(1)} custom-call(f32[8,4,8,128]{3,2,1,0:T(8,128)S(1)} %bitcast.95, f32[8,512,128]{2,1,0:T(8,128)S(1)} %get-tuple-element.12.wide), custom_call_target="tpu_custom_call" | custom-call | flops 33554432 | bytes 1048576 | tf_op jit(solution)/shard_map/kept_half/pallas_call | solution.py:123
  17.6 15.5 %all_to_all.60 = f32[32,1,8,128]{3,2,1,0:T(8,128)S(1)} all-to-all(f32[32,1,8,128]{3,2,1,0:T(8,128)S(1)} %bitcast.97), channel_id=1, replica_groups=mesh['x'=4,'y'=4,'z'=16,'k'=2] {'x','y','k'}, dimensions={0} | all-to-all | bytes 262144 | tf_op jit(solution)/shard_map/all_to_all | solution.py:140
  33.1 25.4 %all_to_all.61 = f32[16,1,8,128]{3,2,1,0:T(8,128)S(1)} all-to-all(f32[16,1,8,128]{3,2,1,0:T(8,128)S(1)} %fusion.7), channel_id=1, replica_groups=mesh['x'=4,'y'=4,'z'=16,'k'=2] {'z'}, dimensions={0} | all-to-all | bytes 131072 | tf_op jit(solution)/shard_map/all_to_all | solution.py:140
  58.6 9.4 %all_to_all.62 = f32[16,2,8,128]{3,2,1,0:T(8,128)S(1)} all-to-all(f32[16,2,8,128]{3,2,1,0:T(8,128)S(1)} %broadcast_in_dim.37), channel_id=1, replica_groups=mesh['x'=4,'y'=4,'z'=16,'k'=2] {'x','y'}, dimensions={0} | all-to-all | bytes 262144 | tf_op jit(solution)/shard_map/all_to_all | solution.py:140
  68.0 5.2 %sent_half.5 = (f32[4,4,2,8,128]{4,3,2,1,0:T(8,128)S(1)}, f32[8,512,128]{2,1,0:T(8,128)S(1)}) custom-call(f32[4,2,8,128]{3,2,1,0:T(8,128)S(1)} %broadcast_in_dim.36.caps_ref, f32[4,4,2,8,128]{4,3,2,1,0:T(8,128)S(1)} %bitcast.90, bf16[4,512,1024]{2,1,0:T(8,128)(2,1)S(1)} %copy-done), custom_call_target="tpu_custom_call" | custom-call | flops 33554432 | bytes 1048576 | tf_op jit(solution)/shard_map/sent_half/pallas_call | solution.py:123
  73.2 2.7 %collective-permute-start.1 = (f32[4,4,2,8,128]{4,3,2,1,0:T(8,128)S(1)}, f32[4,4,2,8,128]{4,3,2,1,0:T(8,128)S(1)}, u32[]{:S(2)}, u32[]{:S(2)}) collective-permute-start(f32[4,4,2,8,128]{4,3,2,1,0:T(8,128)S(1)} %get-tuple-element.15), channel_id=1, source_target_pairs={{0,2},{2,0},{4,6},{6,4},{8,10},{10,8},{12,14},{14,12},{16,18},{18,... | collective-permute-start | bytes 393224 | tf_op jit(solution)/shard_map/ppermute | solution.py:161
  75.9 5.1 %kept_half.5 = f32[4,4,2,8,128]{4,3,2,1,0:T(8,128)S(1)} custom-call(f32[4,4,2,8,128]{4,3,2,1,0:T(8,128)S(1)} %bitcast.91, f32[8,512,128]{2,1,0:T(8,128)S(1)} %get-tuple-element.14.wide), custom_call_target="tpu_custom_call" | custom-call | flops 33554432 | bytes 1048576 | tf_op jit(solution)/shard_map/kept_half/pallas_call | solution.py:123
  81.1 14.8 %all_to_all.63 = f32[32,1,8,128]{3,2,1,0:T(8,128)S(1)} all-to-all(f32[32,1,8,128]{3,2,1,0:T(8,128)S(1)} %bitcast.98), channel_id=1, replica_groups=mesh['x'=4,'y'=4,'z'=16,'k'=2] {'x','y','k'}, dimensions={0} | all-to-all | bytes 262144 | tf_op jit(solution)/shard_map/all_to_all | solution.py:140
  95.9 14.5 %all_to_all.64 = f32[16,1,8,128]{3,2,1,0:T(8,128)S(1)} all-to-all(f32[16,1,8,128]{3,2,1,0:T(8,128)S(1)} %fusion.5), channel_id=1, replica_groups=mesh['x'=4,'y'=4,'z'=16,'k'=2] {'z'}, dimensions={0} | all-to-all | bytes 131072 | tf_op jit(solution)/shard_map/all_to_all | solution.py:140
  110.4 9.4 %all_to_all.65 = f32[16,2,8,128]{3,2,1,0:T(8,128)S(1)} all-to-all(f32[16,2,8,128]{3,2,1,0:T(8,128)S(1)} %broadcast_in_dim.38), channel_id=1, replica_groups=mesh['x'=4,'y'=4,'z'=16,'k'=2] {'x','y'}, dimensions={0} | all-to-all | bytes 262144 | tf_op jit(solution)/shard_map/all_to_all | solution.py:140
  119.8 5.2 %sent_half.6 = (f32[4,4,2,8,128]{4,3,2,1,0:T(8,128)S(1)}, f32[8,512,128]{2,1,0:T(8,128)S(1)}) custom-call(f32[4,2,8,128]{3,2,1,0:T(8,128)S(1)} %broadcast_in_dim.36.caps_ref, f32[4,4,2,8,128]{4,3,2,1,0:T(8,128)S(1)} %bitcast.92, bf16[4,512,1024]{2,1,0:T(8,128)(2,1)S(1)} %copy-done), custom_call_target="tpu_custom_call" | custom-call | flops 33554432 | bytes 1048576 | tf_op jit(solution)/shard_map/sent_half/pallas_call | solution.py:123
  125.1 2.7 %collective-permute-start.2 = (f32[4,4,2,8,128]{4,3,2,1,0:T(8,128)S(1)}, f32[4,4,2,8,128]{4,3,2,1,0:T(8,128)S(1)}, u32[]{:S(2)}, u32[]{:S(2)}) collective-permute-start(f32[4,4,2,8,128]{4,3,2,1,0:T(8,128)S(1)} %get-tuple-element.17), channel_id=1, source_target_pairs={{0,2},{2,0},{4,6},{6,4},{8,10},{10,8},{12,14},{14,12},{16,18},{18,... | collective-permute-start | bytes 393224 | tf_op jit(solution)/shard_map/ppermute | solution.py:161
  127.8 5.1 %kept_half.6 = f32[4,4,2,8,128]{4,3,2,1,0:T(8,128)S(1)} custom-call(f32[4,4,2,8,128]{4,3,2,1,0:T(8,128)S(1)} %bitcast.93, f32[8,512,128]{2,1,0:T(8,128)S(1)} %get-tuple-element.16.wide), custom_call_target="tpu_custom_call" | custom-call | flops 33554432 | bytes 1048576 | tf_op jit(solution)/shard_map/kept_half/pallas_call | solution.py:123
  132.9 14.8 %all_to_all.66 = f32[32,1,8,128]{3,2,1,0:T(8,128)S(1)} all-to-all(f32[32,1,8,128]{3,2,1,0:T(8,128)S(1)} %bitcast.99), channel_id=1, replica_groups=mesh['x'=4,'y'=4,'z'=16,'k'=2] {'x','y','k'}, dimensions={0} | all-to-all | bytes 262144 | tf_op jit(solution)/shard_map/all_to_all | solution.py:140
  147.8 14.5 %all_to_all.67 = f32[16,1,8,128]{3,2,1,0:T(8,128)S(1)} all-to-all(f32[16,1,8,128]{3,2,1,0:T(8,128)S(1)} %fusion.3), channel_id=1, replica_groups=mesh['x'=4,'y'=4,'z'=16,'k'=2] {'z'}, dimensions={0} | all-to-all | bytes 131072 | tf_op jit(solution)/shard_map/all_to_all | solution.py:140
  162.3 9.4 %all_to_all.68 = f32[16,2,8,128]{3,2,1,0:T(8,128)S(1)} all-to-all(f32[16,2,8,128]{3,2,1,0:T(8,128)S(1)} %broadcast_in_dim.39), channel_id=1, replica_groups=mesh['x'=4,'y'=4,'z'=16,'k'=2] {'x','y'}, dimensions={0} | all-to-all | bytes 262144 | tf_op jit(solution)/shard_map/all_to_all | solution.py:140
  171.7 5.2 %sent_half.7 = (f32[4,4,2,8,128]{4,3,2,1,0:T(8,128)S(1)}, f32[8,512,128]{2,1,0:T(8,128)S(1)}) custom-call(f32[4,2,8,128]{3,2,1,0:T(8,128)S(1)} %broadcast_in_dim.36.caps_ref, f32[4,4,2,8,128]{4,3,2,1,0:T(8,128)S(1)} %bitcast.88, bf16[4,512,1024]{2,1,0:T(8,128)(2,1)S(1)} %copy-done), custom_call_target="tpu_custom_call" | custom-call | flops 33554432 | bytes 1048576 | tf_op jit(solution)/shard_map/sent_half/pallas_call | solution.py:123
  176.9 2.7 %collective-permute-start.3 = (f32[4,4,2,8,128]{4,3,2,1,0:T(8,128)S(1)}, f32[4,4,2,8,128]{4,3,2,1,0:T(8,128)S(1)}, u32[]{:S(2)}, u32[]{:S(2)}) collective-permute-start(f32[4,4,2,8,128]{4,3,2,1,0:T(8,128)S(1)} %get-tuple-element.19), channel_id=1, source_target_pairs={{0,2},{2,0},{4,6},{6,4},{8,10},{10,8},{12,14},{14,12},{16,18},{18,... | collective-permute-start | bytes 393224 | tf_op jit(solution)/shard_map/ppermute | solution.py:161
  179.7 5.1 %kept_half.7 = f32[4,4,2,8,128]{4,3,2,1,0:T(8,128)S(1)} custom-call(f32[4,4,2,8,128]{4,3,2,1,0:T(8,128)S(1)} %bitcast.89, f32[8,512,128]{2,1,0:T(8,128)S(1)} %get-tuple-element.18.wide), custom_call_target="tpu_custom_call" | custom-call | flops 33554432 | bytes 1048576 | tf_op jit(solution)/shard_map/kept_half/pallas_call | solution.py:123
  185.0 16.1 %all_to_all.69 = f32[32,2,8,128]{3,2,1,0:T(8,128)S(1)} all-to-all(f32[32,2,8,128]{3,2,1,0:T(8,128)S(1)} %pad_maximum_fusion), channel_id=1, replica_groups=mesh['x'=4,'y'=4,'z'=16,'k'=2] {'x','y','k'}, dimensions={0} | all-to-all | bytes 524288 | tf_op jit(solution)/shard_map/all_to_all | solution.py:140
  201.2 15.0 %all_to_all.70 = f32[16,2,8,128]{3,2,1,0:T(8,128)S(1)} all-to-all(f32[16,2,8,128]{3,2,1,0:T(8,128)S(1)} %pad_maximum_fusion.1), channel_id=1, replica_groups=mesh['x'=4,'y'=4,'z'=16,'k'=2] {'z'}, dimensions={0} | all-to-all | bytes 262144 | tf_op jit(solution)/shard_map/all_to_all | solution.py:140
  216.8 9.4 %all_to_all.71 = f32[16,2,8,128]{3,2,1,0:T(8,128)S(1)} all-to-all(f32[16,2,8,128]{3,2,1,0:T(8,128)S(1)} %broadcast_in_dim.73), channel_id=1, replica_groups=mesh['x'=4,'y'=4,'z'=16,'k'=2] {'x','y'}, dimensions={0} | all-to-all | bytes 262144 | tf_op jit(solution)/shard_map/all_to_all | solution.py:140
  (36 shorter events, 3.9 us)
Async XLA Ops:
  0.6 2.2 copy-start.1
  2.9 65.1 %copy-start = (bf16[4,512,1024]{2,1,0:T(8,128)(2,1)S(1)}, bf16[4,512,1024]{2,1,0:T(8,128)(2,1)}, u32[]{:S(2)}) copy-start(bf16[4,512,1024]{2,1,0:T(8,128)(2,1)} %delay_ref.5) | copy-start | bytes 12582916
  8.1 9.5 %collective-permute-start = (f32[4,4,2,8,128]{4,3,2,1,0:T(8,128)S(1)}, f32[4,4,2,8,128]{4,3,2,1,0:T(8,128)S(1)}, u32[]{:S(2)}, u32[]{:S(2)}) collective-permute-start(f32[4,4,2,8,128]{4,3,2,1,0:T(8,128)S(1)} %get-tuple-element.13), channel_id=1, source_target_pairs={{0,2},{2,0},{4,6},{6,4},{8,10},{10,8},{12,14},{14,12},{16,18},{18,... | collective-permute-start | bytes 393224 | tf_op jit(solution)/shard_map/ppermute | solution.py:161
  73.2 7.9 %collective-permute-start.1 = (f32[4,4,2,8,128]{4,3,2,1,0:T(8,128)S(1)}, f32[4,4,2,8,128]{4,3,2,1,0:T(8,128)S(1)}, u32[]{:S(2)}, u32[]{:S(2)}) collective-permute-start(f32[4,4,2,8,128]{4,3,2,1,0:T(8,128)S(1)} %get-tuple-element.15), channel_id=1, source_target_pairs={{0,2},{2,0},{4,6},{6,4},{8,10},{10,8},{12,14},{14,12},{16,18},{18,... | collective-permute-start | bytes 393224 | tf_op jit(solution)/shard_map/ppermute | solution.py:161
  125.1 7.9 %collective-permute-start.2 = (f32[4,4,2,8,128]{4,3,2,1,0:T(8,128)S(1)}, f32[4,4,2,8,128]{4,3,2,1,0:T(8,128)S(1)}, u32[]{:S(2)}, u32[]{:S(2)}) collective-permute-start(f32[4,4,2,8,128]{4,3,2,1,0:T(8,128)S(1)} %get-tuple-element.17), channel_id=1, source_target_pairs={{0,2},{2,0},{4,6},{6,4},{8,10},{10,8},{12,14},{14,12},{16,18},{18,... | collective-permute-start | bytes 393224 | tf_op jit(solution)/shard_map/ppermute | solution.py:161
  176.9 7.9 %collective-permute-start.3 = (f32[4,4,2,8,128]{4,3,2,1,0:T(8,128)S(1)}, f32[4,4,2,8,128]{4,3,2,1,0:T(8,128)S(1)}, u32[]{:S(2)}, u32[]{:S(2)}) collective-permute-start(f32[4,4,2,8,128]{4,3,2,1,0:T(8,128)S(1)} %get-tuple-element.19), channel_id=1, source_target_pairs={{0,2},{2,0},{4,6},{6,4},{8,10},{10,8},{12,14},{14,12},{16,18},{18,... | collective-permute-start | bytes 393224 | tf_op jit(solution)/shard_map/ppermute | solution.py:161

commit v7 on v6

--- a/solution.py
+++ b/solution.py
@@ -15,52 +15,47 @@
 HALF = 4
 TILES = 4
 SHIFT = 8
-TURNS = 4
+TURNS = 8
+ROTATIONS = LANE // (SHIFT * TURNS)
 
 
-def half_body(times, convert, wide, out_ref, spread_a, spread_b, turned):
-    rotations = LANE // (SHIFT * TURNS)
-    chunk = TILES * SHIFT
+def spread_one(dest, e, q, place, held):
+    a, t, g = place
+    lane = e * SHIFT + a
+    row = (q * 2 + t) * SHIFT + a
+    dest[row, g] = jnp.broadcast_to(held[t, g][:, lane : lane + 1], (SUB, LANE))
 
-    for m in range(rotations):
+
+PLACES = [(a, t, g) for a in range(SHIFT) for t in range(2) for g in range(HALF)]
+
+
+def held_rows(turned, m, q):
+    return {(t, g): turned[m, q * 2 + t, g] for t in range(2) for g in range(HALF)}
+
+
+def fill_turned(times, turned):
+    for m in range(ROTATIONS):
         for tile in range(TILES):
             for g in range(HALF):
                 value = times(g, tile)
                 turned[m, tile, g] = pltpu.roll(value, LANE - m * SHIFT * TURNS, 1) if m else value
-    out_ref[...] = jnp.full(out_ref.shape, EMPTY, jnp.float32)
 
-    def held_rows(m, q):
-        return {(t, g): turned[m, q * 2 + t, g] for t in range(2) for g in range(HALF)}
 
-    def spread_one(dest, e, q, place, held):
-        a, t, g = place
-        lane = e * SHIFT + a
-        row = (q * 2 + t) * SHIFT + a
-        dest[row, g] = jnp.broadcast_to(held[t, g][:, lane : lane + 1], (SUB, LANE))
-
-    places = [(a, t, g) for a in range(SHIFT) for t in range(2) for g in range(HALF)]
-
-    def warm(q, _):
-        held = held_rows(0, q)
-        for place in places:
-            spread_one(spread_a, 0, q, place, held)
-        convert(q)
-        return 0
-
-    for q in range(2):
-        warm(q, 0)
+def half_loop(wide, out_ref, spread_a, spread_b, turned):
+    chunk = TILES * SHIFT
+    final = turned.shape[0] - 1
 
     def stage(m, e, source, dest):
-        next_m = m if e + 1 < TURNS else jnp.minimum(m + 1, rotations - 1)
+        next_m = m if e + 1 < TURNS else jnp.minimum(m + 1, final)
         next_e = (e + 1) % TURNS
 
         def body(q, _):
             side = lax.rem(q, 2)
             late = (q // 2) * HALF
-            held = held_rows(next_m, q)
+            held = held_rows(turned, next_m, q)
             keys = [(g, j) for g in range(HALF) for j in range(4)]
             best = {(g, j): out_ref[g, j, side] for g, j in keys}
-            todo = list(places)
+            todo = list(PLACES)
             for k in range(chunk):
                 place = (k // SHIFT) * LANE + e * SHIFT + k % SHIFT
                 at = pl.ds(m * (SHIFT * TURNS) + place, 1)
@@ -83,7 +78,7 @@
             stage(m, e, *pair)
         return 0
 
-    lax.fori_loop(0, rotations, rotation, 0)
+    lax.fori_loop(0, ROTATIONS, rotation, 0)
 
 
 def times_of(t_ref, half):
@@ -92,48 +87,52 @@
     return lambda g, tile: t_ref[g, tile, half]
 
 
-def parity():
-    return lax.rem(lax.axis_index("z"), 2)
-
-
-def sent_kernel(level, caps_ref, t_ref, delay_ref, out_ref, wide, *scratch):
+def sent_kernel(level, caps_ref, t_ref, delay_ref, out_ref, wide, kept_turned, kept_first, spread_b, turned):
     slab = level if delay_ref.shape[0] > 1 else 0
-
-    def convert(q):
+    odd = lax.rem(lax.axis_index("z"), 2)
+    fill_turned(times_of(t_ref, 1 - odd), turned)
+    fill_turned(times_of(t_ref, odd), kept_turned)
+    for tile in range(TILES):
+        for g in range(HALF):
+            turned[ROTATIONS, tile, g] = times_of(t_ref, odd)(g, tile)
+    out_ref[...] = jnp.full(out_ref.shape, EMPTY, jnp.float32)
+    for q in range(2):
+        held = held_rows(turned, 0, q)
+        for place in PLACES:
+            spread_one(kept_first, 0, q, place, held)
         rows = pl.ds(q * 2 * LANE, 2 * LANE)
         for j in range(8):
             value = delay_ref[slab, rows, j * LANE : (j + 1) * LANE].astype(jnp.float32)
             wide[j, rows, :] = jnp.minimum(value, caps_ref[level, j // 4, 0:1, :])
-
-    half_body(times_of(t_ref, 1 - parity()), convert, wide, out_ref, *scratch)
+    half_loop(wide, out_ref, kept_first, spread_b, turned)
 
 
-def kept_kernel(t_ref, wide, out_ref, *scratch):
-    half_body(times_of(t_ref, parity()), lambda q: None, wide, out_ref, *scratch)
+def kept_kernel(wide, turned, first, out_ref, spread_a, spread_b):
+    out_ref[...] = jnp.full(out_ref.shape, EMPTY, jnp.float32)
+    spread_a[...] = first[...]
+    half_loop(wide, out_ref, spread_a, spread_b, turned)
 
 
-def half_max(level, caps, times, source, shape):
+def half_max(level, operands, shape):
     levels, rows, width = shape
     work = HALF * SUB * rows * width
     vmem = pl.BlockSpec(memory_space=pltpu.VMEM)
     out = jax.ShapeDtypeStruct((HALF, 4, 2, SUB, LANE), jnp.float32)
     wide = jax.ShapeDtypeStruct((width // LANE, rows, LANE), jnp.float32)
-    spread = pltpu.VMEM((TILES * SHIFT, HALF, SUB, LANE), jnp.float32)
+    tall, wider = (ROTATIONS, TILES, HALF, SUB, LANE), (ROTATIONS + 1, TILES, HALF, SUB, LANE)
+    spread = (TILES * SHIFT, HALF, SUB, LANE)
     sent = level is not None
+    outs = (out, wide, jax.ShapeDtypeStruct(tall, jnp.float32), jax.ShapeDtypeStruct(spread, jnp.float32))
     return pl.pallas_call(
         functools.partial(sent_kernel, level) if sent else kept_kernel,
-        out_shape=(out, wide) if sent else out,
-        in_specs=[vmem] * (3 if sent else 2),
-        out_specs=(vmem, vmem) if sent else vmem,
-        scratch_shapes=[
-            spread,
-            spread,
-            pltpu.VMEM((LANE // (SHIFT * TURNS), TILES, HALF, SUB, LANE), jnp.float32),
-        ],
+        out_shape=outs if sent else out,
+        in_specs=[vmem] * 3,
+        out_specs=(vmem,) * 4 if sent else vmem,
+        scratch_shapes=[pltpu.VMEM(spread, jnp.float32), pltpu.VMEM(wider if sent else spread, jnp.float32)],
         compiler_params=pltpu.CompilerParams(vmem_limit_bytes=16 * 1024 * 1024),
         cost_estimate=pl.CostEstimate(flops=2 * work, bytes_accessed=2 * rows * width, transcendentals=0),
         name="sent_half" if sent else "kept_half",
-    )(*((caps, times, source) if sent else (times, source)))
+    )(*operands)
 
 
 def exchange(value, axes):
@@ -157,9 +156,10 @@
     worst = None
     for level in range(levels):
         last = level == levels - 1
-        sent, wide = half_max(level, caps, times, delay[:1] if level == 0 else delay, delay.shape)
+        source = delay[:1] if level == 0 else delay
+        sent, *shared = half_max(level, (caps, times, source), delay.shape)
         got = lax.ppermute(sent, "z", neighbour)
-        kept = half_max(None, None, times, wide, delay.shape)
+        kept = half_max(None, shared, delay.shape)
         best = jnp.maximum(kept, got)
         parts = best.reshape(plane * 2, 1, SUB, LANE)
         if last:

time: 230 us -> 229 us (level)
  no operation moved by 1% of the time
where the time goes in v7:
time: 229 us; the launch traced here: 226 us
  blocking collectives  168 us (73%)
  Pallas kernels  40.1 us (18%)
  starting transfers between devices  12.6 us (6%)
    all_to_all x12, blocking collectives, exchange(): return lax.all_to_all(value, axes, split_axis=0, concat_axis=0, tiled=True)  168 us
    pallas_call x8, Pallas kernels, half_max(): pl.pallas_call(functools.partial(sent_kernel, level) if sent else kept_ke...  40.1 us
    ppermute x4, starting transfers between devices, shards(): got = lax.ppermute(sent, 'z', neighbour)  12.6 us
  transfers between devices with their start and end apart: 4, of which 0 were waited for; matrix products, arithmetic and copies ran while one was open for 0% of the time, Pallas kernels for 9%

profile of v7, /device:TPU:1, one launch (start us, length us, event | category | flops | bytes accessed | tf_op | source)
XLA Modules:
  0.0 225.8 jit_solution(4118442614555706062)
XLA Ops:
  2.9 5.2 %sent_half.4 = (f32[4,4,2,8,128]{4,3,2,1,0:T(8,128)S(1)}, f32[8,512,128]{2,1,0:T(8,128)S(1)}, f32[2,4,4,8,128]{4,3,2,1,0:T(8,128)S(1)}, f32[32,4,8,128]{3,2,1,0:T(8,128)S(1)}) custom-call(f32[4,2,8,128]{3,2,1,0:T(8,128)S(1)} %broadcast_in_dim.36.caps_ref, f32[8,4,8,128]{3,2,1,0:T(8,128)S(1)} %bitcast.91, bf16[1,512,1024]{2,1,0:T(8,128)(2,1)S(1)} %slice.42.delay_ref), custom_call_target="tpu_custom_call" | custom-call | flops 33554432 | bytes 1048576 | tf_op jit(solution)/shard_map/sent_half/pallas_call | solution.py:126
  8.0 4.4 %collective-permute-start = (f32[4,4,2,8,128]{4,3,2,1,0:T(8,128)S(1)}, f32[4,4,2,8,128]{4,3,2,1,0:T(8,128)S(1)}, u32[]{:S(2)}, u32[]{:S(2)}) collective-permute-start(f32[4,4,2,8,128]{4,3,2,1,0:T(8,128)S(1)} %get-tuple-element.23), channel_id=1, source_target_pairs={{0,2},{2,0},{4,6},{6,4},{8,10},{10,8},{12,14},{14,12},{16,18},{18,... | collective-permute-start | bytes 393224 | tf_op jit(solution)/shard_map/ppermute | solution.py:161
  12.4 4.8 %kept_half.4 = f32[4,4,2,8,128]{4,3,2,1,0:T(8,128)S(1)} custom-call(f32[8,512,128]{2,1,0:T(8,128)S(1)} %get-tuple-element.20.wide, f32[2,4,4,8,128]{4,3,2,1,0:T(8,128)S(1)} %get-tuple-element.21.turned, f32[32,4,8,128]{3,2,1,0:T(8,128)S(1)} %get-tuple-element.22.first), custom_call_target="tpu_custom_call" | custom-call | flops 33554432 | bytes 1048576 | tf_op jit(solution)/shard_map/kept_half/pallas_call | solution.py:126
  17.3 15.5 %all_to_all.60 = f32[32,1,8,128]{3,2,1,0:T(8,128)S(1)} all-to-all(f32[32,1,8,128]{3,2,1,0:T(8,128)S(1)} %bitcast.93), channel_id=1, replica_groups=mesh['x'=4,'y'=4,'z'=16,'k'=2] {'x','y','k'}, dimensions={0} | all-to-all | bytes 262144 | tf_op jit(solution)/shard_map/all_to_all | solution.py:139
  32.8 25.4 %all_to_all.61 = f32[16,1,8,128]{3,2,1,0:T(8,128)S(1)} all-to-all(f32[16,1,8,128]{3,2,1,0:T(8,128)S(1)} %fusion.7), channel_id=1, replica_groups=mesh['x'=4,'y'=4,'z'=16,'k'=2] {'z'}, dimensions={0} | all-to-all | bytes 131072 | tf_op jit(solution)/shard_map/all_to_all | solution.py:139
  58.3 9.4 %all_to_all.62 = f32[16,2,8,128]{3,2,1,0:T(8,128)S(1)} all-to-all(f32[16,2,8,128]{3,2,1,0:T(8,128)S(1)} %broadcast_in_dim.37), channel_id=1, replica_groups=mesh['x'=4,'y'=4,'z'=16,'k'=2] {'x','y'}, dimensions={0} | all-to-all | bytes 262144 | tf_op jit(solution)/shard_map/all_to_all | solution.py:139
  67.7 5.2 %sent_half.5 = (f32[4,4,2,8,128]{4,3,2,1,0:T(8,128)S(1)}, f32[8,512,128]{2,1,0:T(8,128)S(1)}, f32[2,4,4,8,128]{4,3,2,1,0:T(8,128)S(1)}, f32[32,4,8,128]{3,2,1,0:T(8,128)S(1)}) custom-call(f32[4,2,8,128]{3,2,1,0:T(8,128)S(1)} %broadcast_in_dim.36.caps_ref, f32[4,4,2,8,128]{4,3,2,1,0:T(8,128)S(1)} %bitcast.89, bf16[4,512,1024]{2,1,0:T(8,128)(2,1)S(1)} %copy-done), custom_call_target="tpu_custom_call" | custom-call | flops 33554432 | bytes 1048576 | tf_op jit(solution)/shard_map/sent_half/pallas_call | solution.py:126
  72.9 2.7 %collective-permute-start.1 = (f32[4,4,2,8,128]{4,3,2,1,0:T(8,128)S(1)}, f32[4,4,2,8,128]{4,3,2,1,0:T(8,128)S(1)}, u32[]{:S(2)}, u32[]{:S(2)}) collective-permute-start(f32[4,4,2,8,128]{4,3,2,1,0:T(8,128)S(1)} %get-tuple-element.27), channel_id=1, source_target_pairs={{0,2},{2,0},{4,6},{6,4},{8,10},{10,8},{12,14},{14,12},{16,18},{18,... | collective-permute-start | bytes 393224 | tf_op jit(solution)/shard_map/ppermute | solution.py:161
  75.6 4.8 %kept_half.5 = f32[4,4,2,8,128]{4,3,2,1,0:T(8,128)S(1)} custom-call(f32[8,512,128]{2,1,0:T(8,128)S(1)} %get-tuple-element.24.wide, f32[2,4,4,8,128]{4,3,2,1,0:T(8,128)S(1)} %get-tuple-element.25.turned, f32[32,4,8,128]{3,2,1,0:T(8,128)S(1)} %get-tuple-element.26.first), custom_call_target="tpu_custom_call" | custom-call | flops 33554432 | bytes 1048576 | tf_op jit(solution)/shard_map/kept_half/pallas_call | solution.py:126
  80.5 14.8 %all_to_all.63 = f32[32,1,8,128]{3,2,1,0:T(8,128)S(1)} all-to-all(f32[32,1,8,128]{3,2,1,0:T(8,128)S(1)} %bitcast.94), channel_id=1, replica_groups=mesh['x'=4,'y'=4,'z'=16,'k'=2] {'x','y','k'}, dimensions={0} | all-to-all | bytes 262144 | tf_op jit(solution)/shard_map/all_to_all | solution.py:139
  95.3 14.5 %all_to_all.64 = f32[16,1,8,128]{3,2,1,0:T(8,128)S(1)} all-to-all(f32[16,1,8,128]{3,2,1,0:T(8,128)S(1)} %fusion.5), channel_id=1, replica_groups=mesh['x'=4,'y'=4,'z'=16,'k'=2] {'z'}, dimensions={0} | all-to-all | bytes 131072 | tf_op jit(solution)/shard_map/all_to_all | solution.py:139
  109.9 9.4 %all_to_all.65 = f32[16,2,8,128]{3,2,1,0:T(8,128)S(1)} all-to-all(f32[16,2,8,128]{3,2,1,0:T(8,128)S(1)} %broadcast_in_dim.38), channel_id=1, replica_groups=mesh['x'=4,'y'=4,'z'=16,'k'=2] {'x','y'}, dimensions={0} | all-to-all | bytes 262144 | tf_op jit(solution)/shard_map/all_to_all | solution.py:139
  119.3 5.2 %sent_half.6 = (f32[4,4,2,8,128]{4,3,2,1,0:T(8,128)S(1)}, f32[8,512,128]{2,1,0:T(8,128)S(1)}, f32[2,4,4,8,128]{4,3,2,1,0:T(8,128)S(1)}, f32[32,4,8,128]{3,2,1,0:T(8,128)S(1)}) custom-call(f32[4,2,8,128]{3,2,1,0:T(8,128)S(1)} %broadcast_in_dim.36.caps_ref, f32[4,4,2,8,128]{4,3,2,1,0:T(8,128)S(1)} %bitcast.90, bf16[4,512,1024]{2,1,0:T(8,128)(2,1)S(1)} %copy-done), custom_call_target="tpu_custom_call" | custom-call | flops 33554432 | bytes 1048576 | tf_op jit(solution)/shard_map/sent_half/pallas_call | solution.py:126
  124.5 2.7 %collective-permute-start.2 = (f32[4,4,2,8,128]{4,3,2,1,0:T(8,128)S(1)}, f32[4,4,2,8,128]{4,3,2,1,0:T(8,128)S(1)}, u32[]{:S(2)}, u32[]{:S(2)}) collective-permute-start(f32[4,4,2,8,128]{4,3,2,1,0:T(8,128)S(1)} %get-tuple-element.31), channel_id=1, source_target_pairs={{0,2},{2,0},{4,6},{6,4},{8,10},{10,8},{12,14},{14,12},{16,18},{18,... | collective-permute-start | bytes 393224 | tf_op jit(solution)/shard_map/ppermute | solution.py:161
  127.2 4.8 %kept_half.6 = f32[4,4,2,8,128]{4,3,2,1,0:T(8,128)S(1)} custom-call(f32[8,512,128]{2,1,0:T(8,128)S(1)} %get-tuple-element.28.wide, f32[2,4,4,8,128]{4,3,2,1,0:T(8,128)S(1)} %get-tuple-element.29.turned, f32[32,4,8,128]{3,2,1,0:T(8,128)S(1)} %get-tuple-element.30.first), custom_call_target="tpu_custom_call" | custom-call | flops 33554432 | bytes 1048576 | tf_op jit(solution)/shard_map/kept_half/pallas_call | solution.py:126
  132.1 14.8 %all_to_all.66 = f32[32,1,8,128]{3,2,1,0:T(8,128)S(1)} all-to-all(f32[32,1,8,128]{3,2,1,0:T(8,128)S(1)} %bitcast.95), channel_id=1, replica_groups=mesh['x'=4,'y'=4,'z'=16,'k'=2] {'x','y','k'}, dimensions={0} | all-to-all | bytes 262144 | tf_op jit(solution)/shard_map/all_to_all | solution.py:139
  146.9 14.5 %all_to_all.67 = f32[16,1,8,128]{3,2,1,0:T(8,128)S(1)} all-to-all(f32[16,1,8,128]{3,2,1,0:T(8,128)S(1)} %fusion.3), channel_id=1, replica_groups=mesh['x'=4,'y'=4,'z'=16,'k'=2] {'z'}, dimensions={0} | all-to-all | bytes 131072 | tf_op jit(solution)/shard_map/all_to_all | solution.py:139
  161.5 9.4 %all_to_all.68 = f32[16,2,8,128]{3,2,1,0:T(8,128)S(1)} all-to-all(f32[16,2,8,128]{3,2,1,0:T(8,128)S(1)} %broadcast_in_dim.39), channel_id=1, replica_groups=mesh['x'=4,'y'=4,'z'=16,'k'=2] {'x','y'}, dimensions={0} | all-to-all | bytes 262144 | tf_op jit(solution)/shard_map/all_to_all | solution.py:139
  170.9 5.2 %sent_half.7 = (f32[4,4,2,8,128]{4,3,2,1,0:T(8,128)S(1)}, f32[8,512,128]{2,1,0:T(8,128)S(1)}, f32[2,4,4,8,128]{4,3,2,1,0:T(8,128)S(1)}, f32[32,4,8,128]{3,2,1,0:T(8,128)S(1)}) custom-call(f32[4,2,8,128]{3,2,1,0:T(8,128)S(1)} %broadcast_in_dim.36.caps_ref, f32[4,4,2,8,128]{4,3,2,1,0:T(8,128)S(1)} %bitcast.88, bf16[4,512,1024]{2,1,0:T(8,128)(2,1)S(1)} %copy-done), custom_call_target="tpu_custom_call" | custom-call | flops 33554432 | bytes 1048576 | tf_op jit(solution)/shard_map/sent_half/pallas_call | solution.py:126
  176.1 2.7 %collective-permute-start.3 = (f32[4,4,2,8,128]{4,3,2,1,0:T(8,128)S(1)}, f32[4,4,2,8,128]{4,3,2,1,0:T(8,128)S(1)}, u32[]{:S(2)}, u32[]{:S(2)}) collective-permute-start(f32[4,4,2,8,128]{4,3,2,1,0:T(8,128)S(1)} %get-tuple-element.35), channel_id=1, source_target_pairs={{0,2},{2,0},{4,6},{6,4},{8,10},{10,8},{12,14},{14,12},{16,18},{18,... | collective-permute-start | bytes 393224 | tf_op jit(solution)/shard_map/ppermute | solution.py:161
  178.8 4.8 %kept_half.7 = f32[4,4,2,8,128]{4,3,2,1,0:T(8,128)S(1)} custom-call(f32[8,512,128]{2,1,0:T(8,128)S(1)} %get-tuple-element.32.wide, f32[2,4,4,8,128]{4,3,2,1,0:T(8,128)S(1)} %get-tuple-element.33.turned, f32[32,4,8,128]{3,2,1,0:T(8,128)S(1)} %get-tuple-element.34.first), custom_call_target="tpu_custom_call" | custom-call | flops 33554432 | bytes 1048576 | tf_op jit(solution)/shard_map/kept_half/pallas_call | solution.py:126
  183.9 16.1 %all_to_all.69 = f32[32,2,8,128]{3,2,1,0:T(8,128)S(1)} all-to-all(f32[32,2,8,128]{3,2,1,0:T(8,128)S(1)} %pad_maximum_fusion), channel_id=1, replica_groups=mesh['x'=4,'y'=4,'z'=16,'k'=2] {'x','y','k'}, dimensions={0} | all-to-all | bytes 524288 | tf_op jit(solution)/shard_map/all_to_all | solution.py:139
  200.1 15.0 %all_to_all.70 = f32[16,2,8,128]{3,2,1,0:T(8,128)S(1)} all-to-all(f32[16,2,8,128]{3,2,1,0:T(8,128)S(1)} %pad_maximum_fusion.1), channel_id=1, replica_groups=mesh['x'=4,'y'=4,'z'=16,'k'=2] {'z'}, dimensions={0} | all-to-all | bytes 262144 | tf_op jit(solution)/shard_map/all_to_all | solution.py:139
  215.7 9.4 %all_to_all.71 = f32[16,2,8,128]{3,2,1,0:T(8,128)S(1)} all-to-all(f32[16,2,8,128]{3,2,1,0:T(8,128)S(1)} %broadcast_in_dim.73), channel_id=1, replica_groups=mesh['x'=4,'y'=4,'z'=16,'k'=2] {'x','y'}, dimensions={0} | all-to-all | bytes 262144 | tf_op jit(solution)/shard_map/all_to_all | solution.py:139
  (36 shorter events, 3.9 us)
Async XLA Ops:
  0.6 2.2 copy-start.1
  8.0 9.2 %collective-permute-start = (f32[4,4,2,8,128]{4,3,2,1,0:T(8,128)S(1)}, f32[4,4,2,8,128]{4,3,2,1,0:T(8,128)S(1)}, u32[]{:S(2)}, u32[]{:S(2)}) collective-permute-start(f32[4,4,2,8,128]{4,3,2,1,0:T(8,128)S(1)} %get-tuple-element.23), channel_id=1, source_target_pairs={{0,2},{2,0},{4,6},{6,4},{8,10},{10,8},{12,14},{14,12},{16,18},{18,... | collective-permute-start | bytes 393224 | tf_op jit(solution)/shard_map/ppermute | solution.py:161
  12.4 55.3 %copy-start = (bf16[4,512,1024]{2,1,0:T(8,128)(2,1)S(1)}, bf16[4,512,1024]{2,1,0:T(8,128)(2,1)}, u32[]{:S(2)}) copy-start(bf16[4,512,1024]{2,1,0:T(8,128)(2,1)} %delay_ref.5) | copy-start | bytes 12582916
  72.9 7.6 %collective-permute-start.1 = (f32[4,4,2,8,128]{4,3,2,1,0:T(8,128)S(1)}, f32[4,4,2,8,128]{4,3,2,1,0:T(8,128)S(1)}, u32[]{:S(2)}, u32[]{:S(2)}) collective-permute-start(f32[4,4,2,8,128]{4,3,2,1,0:T(8,128)S(1)} %get-tuple-element.27), channel_id=1, source_target_pairs={{0,2},{2,0},{4,6},{6,4},{8,10},{10,8},{12,14},{14,12},{16,18},{18,... | collective-permute-start | bytes 393224 | tf_op jit(solution)/shard_map/ppermute | solution.py:161
  124.5 7.6 %collective-permute-start.2 = (f32[4,4,2,8,128]{4,3,2,1,0:T(8,128)S(1)}, f32[4,4,2,8,128]{4,3,2,1,0:T(8,128)S(1)}, u32[]{:S(2)}, u32[]{:S(2)}) collective-permute-start(f32[4,4,2,8,128]{4,3,2,1,0:T(8,128)S(1)} %get-tuple-element.31), channel_id=1, source_target_pairs={{0,2},{2,0},{4,6},{6,4},{8,10},{10,8},{12,14},{14,12},{16,18},{18,... | collective-permute-start | bytes 393224 | tf_op jit(solution)/shard_map/ppermute | solution.py:161
  176.1 7.6 %collective-permute-start.3 = (f32[4,4,2,8,128]{4,3,2,1,0:T(8,128)S(1)}, f32[4,4,2,8,128]{4,3,2,1,0:T(8,128)S(1)}, u32[]{:S(2)}, u32[]{:S(2)}) collective-permute-start(f32[4,4,2,8,128]{4,3,2,1,0:T(8,128)S(1)} %get-tuple-element.35), channel_id=1, source_target_pairs={{0,2},{2,0},{4,6},{6,4},{8,10},{10,8},{12,14},{14,12},{16,18},{18,... | collective-permute-start | bytes 393224 | tf_op jit(solution)/shard_map/ppermute | solution.py:161

commit v8 on v7

--- a/solution.py
+++ b/solution.py
@@ -87,6 +87,20 @@
     return lambda g, tile: t_ref[g, tile, half]
 
 
+def first_kernel(occupancy_ref, t_ref, delay_ref, out_ref, wide, kept_turned, kept_first, caps_ref, *scratch):
+    place = lax.axis_index("x") * lax.axis_size("y") + lax.axis_index("y")
+    col = lax.axis_index("z") * lax.axis_size("k") + lax.axis_index("k")
+    levels, _, width = occupancy_ref.shape
+    lane = lax.broadcasted_iota(jnp.int32, (1, width), 1)
+    for level in range(levels):
+        row = occupancy_ref[level, pl.ds(col, 1), :].astype(jnp.float32)
+        for side in range(2):
+            flag = jnp.max(jnp.where(lane == place * 2 + side, row, 0.0), axis=1, keepdims=True)
+            cap = jnp.where(flag > 0.0, jnp.float32(BOUND), jnp.float32(EMPTY))
+            caps_ref[level, side] = jnp.broadcast_to(cap, (SUB, LANE))
+    sent_kernel(0, caps_ref, t_ref, delay_ref, out_ref, wide, kept_turned, kept_first, *scratch)
+
+
 def sent_kernel(level, caps_ref, t_ref, delay_ref, out_ref, wide, kept_turned, kept_first, spread_b, turned):
     slab = level if delay_ref.shape[0] > 1 else 0
     odd = lax.rem(lax.axis_index("z"), 2)
@@ -123,11 +137,15 @@
     spread = (TILES * SHIFT, HALF, SUB, LANE)
     sent = level is not None
     outs = (out, wide, jax.ShapeDtypeStruct(tall, jnp.float32), jax.ShapeDtypeStruct(spread, jnp.float32))
+    kernel = functools.partial(sent_kernel, level) if sent else kept_kernel
+    if level == 0:
+        kernel = first_kernel
+        outs += (jax.ShapeDtypeStruct((levels, 2, SUB, LANE), jnp.float32),)
     return pl.pallas_call(
-        functools.partial(sent_kernel, level) if sent else kept_kernel,
+        kernel,
         out_shape=outs if sent else out,
         in_specs=[vmem] * 3,
-        out_specs=(vmem,) * 4 if sent else vmem,
+        out_specs=(vmem,) * len(outs) if sent else vmem,
         scratch_shapes=[pltpu.VMEM(spread, jnp.float32), pltpu.VMEM(wider if sent else spread, jnp.float32)],
         compiler_params=pltpu.CompilerParams(vmem_limit_bytes=16 * 1024 * 1024),
         cost_estimate=pl.CostEstimate(flops=2 * work, bytes_accessed=2 * rows * width, transcendentals=0),
@@ -144,12 +162,8 @@
     levels = delay.shape[0]
     plane = lax.axis_size("x") * lax.axis_size("y")
     depth = lax.axis_size("z")
-    place = lax.axis_index("x") * lax.axis_size("y") + lax.axis_index("y")
     odd = lax.axis_index("z") % 2
-    col = lax.axis_index("z") * lax.axis_size("k") + lax.axis_index("k")
-    flags = lax.dynamic_slice(occupancy, (0, col, place * 2), (levels, 1, 2))[:, 0, :]
-    caps = jnp.where(flags > 0, jnp.float32(BOUND), jnp.float32(EMPTY))
-    caps = jnp.broadcast_to(caps[:, :, None, None], (levels, 2, SUB, LANE))
+    caps = occupancy
     groups, tiles = scenarios // SUB, pins // LANE
     neighbour = [(z, z ^ 1) for z in range(depth)]
     times = jnp.transpose(arrival.reshape(groups, SUB, tiles, LANE), (0, 2, 1, 3))
@@ -158,6 +172,8 @@
         last = level == levels - 1
         source = delay[:1] if level == 0 else delay
         sent, *shared = half_max(level, (caps, times, source), delay.shape)
+        if level == 0:
+            caps = shared.pop()
         got = lax.ppermute(sent, "z", neighbour)
         kept = half_max(None, shared, delay.shape)
         best = jnp.maximum(kept, got)

time: 229 us -> 228 us (level)
  no operation moved by 1% of the time
where the time goes in v8:
time: 228 us; the launch traced here: 225 us
  blocking collectives  168 us (74%)
  Pallas kernels  40.1 us (18%)
  starting transfers between devices  12.6 us (6%)
    all_to_all x12, blocking collectives, exchange(): return lax.all_to_all(value, axes, split_axis=0, concat_axis=0, tiled=True)  168 us
    pallas_call x8, Pallas kernels, half_max(): pl.pallas_call(kernel, out_shape=outs if sent else out, in_specs=[vmem] *...  40.1 us
    ppermute x4, starting transfers between devices, shards(): got = lax.ppermute(sent, 'z', neighbour)  12.6 us
  transfers between devices with their start and end apart: 4, of which 0 were waited for; matrix products, arithmetic and copies ran while one was open for 0% of the time, Pallas kernels for 9%

profile of v8, /device:TPU:1, one launch (start us, length us, event | category | flops | bytes accessed | tf_op | source)
XLA Modules:
  0.0 225.0 jit_solution(1771591813496586930)
XLA Ops:
  2.0 5.2 %sent_half.4 = (f32[4,4,2,8,128]{4,3,2,1,0:T(8,128)S(1)}, f32[8,512,128]{2,1,0:T(8,128)S(1)}, f32[2,4,4,8,128]{4,3,2,1,0:T(8,128)S(1)}, f32[32,4,8,128]{3,2,1,0:T(8,128)S(1)}, f32[4,2,8,128]{3,2,1,0:T(8,128)S(1)}) custom-call(s32[4,32,32]{2,1,0:T(8,128)S(1)} %copy-done.2, f32[8,4,8,128]{3,2,1,0:T(8,128)S(1)} %bitcast.90, ...), custom_call_target="tpu_custom_call" | custom-call | flops 33554432 | bytes 1048576 | tf_op jit(solution)/shard_map/sent_half/pallas_call | solution.py:144
  7.2 4.4 %collective-permute-start = (f32[4,4,2,8,128]{4,3,2,1,0:T(8,128)S(1)}, f32[4,4,2,8,128]{4,3,2,1,0:T(8,128)S(1)}, u32[]{:S(2)}, u32[]{:S(2)}) collective-permute-start(f32[4,4,2,8,128]{4,3,2,1,0:T(8,128)S(1)} %get-tuple-element.25), channel_id=1, source_target_pairs={{0,2},{2,0},{4,6},{6,4},{8,10},{10,8},{12,14},{14,12},{16,18},{18,... | collective-permute-start | bytes 393224 | tf_op jit(solution)/shard_map/ppermute | solution.py:177
  11.6 4.8 %kept_half.4 = f32[4,4,2,8,128]{4,3,2,1,0:T(8,128)S(1)} custom-call(f32[8,512,128]{2,1,0:T(8,128)S(1)} %get-tuple-element.22.wide, f32[2,4,4,8,128]{4,3,2,1,0:T(8,128)S(1)} %get-tuple-element.23.turned, f32[32,4,8,128]{3,2,1,0:T(8,128)S(1)} %get-tuple-element.24.first), custom_call_target="tpu_custom_call" | custom-call | flops 33554432 | bytes 1048576 | tf_op jit(solution)/shard_map/kept_half/pallas_call | solution.py:144
  16.5 15.5 %all_to_all.60 = f32[32,1,8,128]{3,2,1,0:T(8,128)S(1)} all-to-all(f32[32,1,8,128]{3,2,1,0:T(8,128)S(1)} %bitcast.92), channel_id=1, replica_groups=mesh['x'=4,'y'=4,'z'=16,'k'=2] {'x','y','k'}, dimensions={0} | all-to-all | bytes 262144 | tf_op jit(solution)/shard_map/all_to_all | solution.py:157
  32.0 25.4 %all_to_all.61 = f32[16,1,8,128]{3,2,1,0:T(8,128)S(1)} all-to-all(f32[16,1,8,128]{3,2,1,0:T(8,128)S(1)} %fusion.7), channel_id=1, replica_groups=mesh['x'=4,'y'=4,'z'=16,'k'=2] {'z'}, dimensions={0} | all-to-all | bytes 131072 | tf_op jit(solution)/shard_map/all_to_all | solution.py:157
  57.5 9.4 %all_to_all.62 = f32[16,2,8,128]{3,2,1,0:T(8,128)S(1)} all-to-all(f32[16,2,8,128]{3,2,1,0:T(8,128)S(1)} %broadcast_in_dim.24), channel_id=1, replica_groups=mesh['x'=4,'y'=4,'z'=16,'k'=2] {'x','y'}, dimensions={0} | all-to-all | bytes 262144 | tf_op jit(solution)/shard_map/all_to_all | solution.py:157
  66.9 5.2 %sent_half.5 = (f32[4,4,2,8,128]{4,3,2,1,0:T(8,128)S(1)}, f32[8,512,128]{2,1,0:T(8,128)S(1)}, f32[2,4,4,8,128]{4,3,2,1,0:T(8,128)S(1)}, f32[32,4,8,128]{3,2,1,0:T(8,128)S(1)}) custom-call(f32[4,2,8,128]{3,2,1,0:T(8,128)S(1)} %get-tuple-element.21.caps_ref, f32[4,4,2,8,128]{4,3,2,1,0:T(8,128)S(1)} %bitcast.87, bf16[4,512,1024]{2,1,0:T(8,128)(2,1)S(1)} %copy-done), custom_call_target="tpu_custom_call" | custom-call | flops 33554432 | bytes 1048576 | tf_op jit(solution)/shard_map/sent_half/pallas_call | solution.py:144
  72.1 2.7 %collective-permute-start.1 = (f32[4,4,2,8,128]{4,3,2,1,0:T(8,128)S(1)}, f32[4,4,2,8,128]{4,3,2,1,0:T(8,128)S(1)}, u32[]{:S(2)}, u32[]{:S(2)}) collective-permute-start(f32[4,4,2,8,128]{4,3,2,1,0:T(8,128)S(1)} %get-tuple-element.29), channel_id=1, source_target_pairs={{0,2},{2,0},{4,6},{6,4},{8,10},{10,8},{12,14},{14,12},{16,18},{18,... | collective-permute-start | bytes 393224 | tf_op jit(solution)/shard_map/ppermute | solution.py:177
  74.8 4.8 %kept_half.5 = f32[4,4,2,8,128]{4,3,2,1,0:T(8,128)S(1)} custom-call(f32[8,512,128]{2,1,0:T(8,128)S(1)} %get-tuple-element.26.wide, f32[2,4,4,8,128]{4,3,2,1,0:T(8,128)S(1)} %get-tuple-element.27.turned, f32[32,4,8,128]{3,2,1,0:T(8,128)S(1)} %get-tuple-element.28.first), custom_call_target="tpu_custom_call" | custom-call | flops 33554432 | bytes 1048576 | tf_op jit(solution)/shard_map/kept_half/pallas_call | solution.py:144
  79.7 14.8 %all_to_all.63 = f32[32,1,8,128]{3,2,1,0:T(8,128)S(1)} all-to-all(f32[32,1,8,128]{3,2,1,0:T(8,128)S(1)} %bitcast.93), channel_id=1, replica_groups=mesh['x'=4,'y'=4,'z'=16,'k'=2] {'x','y','k'}, dimensions={0} | all-to-all | bytes 262144 | tf_op jit(solution)/shard_map/all_to_all | solution.py:157
  94.5 14.5 %all_to_all.64 = f32[16,1,8,128]{3,2,1,0:T(8,128)S(1)} all-to-all(f32[16,1,8,128]{3,2,1,0:T(8,128)S(1)} %fusion.5), channel_id=1, replica_groups=mesh['x'=4,'y'=4,'z'=16,'k'=2] {'z'}, dimensions={0} | all-to-all | bytes 131072 | tf_op jit(solution)/shard_map/all_to_all | solution.py:157
  109.1 9.4 %all_to_all.65 = f32[16,2,8,128]{3,2,1,0:T(8,128)S(1)} all-to-all(f32[16,2,8,128]{3,2,1,0:T(8,128)S(1)} %broadcast_in_dim.25), channel_id=1, replica_groups=mesh['x'=4,'y'=4,'z'=16,'k'=2] {'x','y'}, dimensions={0} | all-to-all | bytes 262144 | tf_op jit(solution)/shard_map/all_to_all | solution.py:157
  118.5 5.2 %sent_half.6 = (f32[4,4,2,8,128]{4,3,2,1,0:T(8,128)S(1)}, f32[8,512,128]{2,1,0:T(8,128)S(1)}, f32[2,4,4,8,128]{4,3,2,1,0:T(8,128)S(1)}, f32[32,4,8,128]{3,2,1,0:T(8,128)S(1)}) custom-call(f32[4,2,8,128]{3,2,1,0:T(8,128)S(1)} %get-tuple-element.21.caps_ref, f32[4,4,2,8,128]{4,3,2,1,0:T(8,128)S(1)} %bitcast.89, bf16[4,512,1024]{2,1,0:T(8,128)(2,1)S(1)} %copy-done), custom_call_target="tpu_custom_call" | custom-call | flops 33554432 | bytes 1048576 | tf_op jit(solution)/shard_map/sent_half/pallas_call | solution.py:144
  123.7 2.7 %collective-permute-start.2 = (f32[4,4,2,8,128]{4,3,2,1,0:T(8,128)S(1)}, f32[4,4,2,8,128]{4,3,2,1,0:T(8,128)S(1)}, u32[]{:S(2)}, u32[]{:S(2)}) collective-permute-start(f32[4,4,2,8,128]{4,3,2,1,0:T(8,128)S(1)} %get-tuple-element.33), channel_id=1, source_target_pairs={{0,2},{2,0},{4,6},{6,4},{8,10},{10,8},{12,14},{14,12},{16,18},{18,... | collective-permute-start | bytes 393224 | tf_op jit(solution)/shard_map/ppermute | solution.py:177
  126.4 4.8 %kept_half.6 = f32[4,4,2,8,128]{4,3,2,1,0:T(8,128)S(1)} custom-call(f32[8,512,128]{2,1,0:T(8,128)S(1)} %get-tuple-element.30.wide, f32[2,4,4,8,128]{4,3,2,1,0:T(8,128)S(1)} %get-tuple-element.31.turned, f32[32,4,8,128]{3,2,1,0:T(8,128)S(1)} %get-tuple-element.32.first), custom_call_target="tpu_custom_call" | custom-call | flops 33554432 | bytes 1048576 | tf_op jit(solution)/shard_map/kept_half/pallas_call | solution.py:144
  131.3 14.8 %all_to_all.66 = f32[32,1,8,128]{3,2,1,0:T(8,128)S(1)} all-to-all(f32[32,1,8,128]{3,2,1,0:T(8,128)S(1)} %bitcast.94), channel_id=1, replica_groups=mesh['x'=4,'y'=4,'z'=16,'k'=2] {'x','y','k'}, dimensions={0} | all-to-all | bytes 262144 | tf_op jit(solution)/shard_map/all_to_all | solution.py:157
  146.1 14.5 %all_to_all.67 = f32[16,1,8,128]{3,2,1,0:T(8,128)S(1)} all-to-all(f32[16,1,8,128]{3,2,1,0:T(8,128)S(1)} %fusion.3), channel_id=1, replica_groups=mesh['x'=4,'y'=4,'z'=16,'k'=2] {'z'}, dimensions={0} | all-to-all | bytes 131072 | tf_op jit(solution)/shard_map/all_to_all | solution.py:157
  160.7 9.4 %all_to_all.68 = f32[16,2,8,128]{3,2,1,0:T(8,128)S(1)} all-to-all(f32[16,2,8,128]{3,2,1,0:T(8,128)S(1)} %broadcast_in_dim.26), channel_id=1, replica_groups=mesh['x'=4,'y'=4,'z'=16,'k'=2] {'x','y'}, dimensions={0} | all-to-all | bytes 262144 | tf_op jit(solution)/shard_map/all_to_all | solution.py:157
  170.1 5.2 %sent_half.7 = (f32[4,4,2,8,128]{4,3,2,1,0:T(8,128)S(1)}, f32[8,512,128]{2,1,0:T(8,128)S(1)}, f32[2,4,4,8,128]{4,3,2,1,0:T(8,128)S(1)}, f32[32,4,8,128]{3,2,1,0:T(8,128)S(1)}) custom-call(f32[4,2,8,128]{3,2,1,0:T(8,128)S(1)} %get-tuple-element.21.caps_ref, f32[4,4,2,8,128]{4,3,2,1,0:T(8,128)S(1)} %bitcast.88, bf16[4,512,1024]{2,1,0:T(8,128)(2,1)S(1)} %copy-done), custom_call_target="tpu_custom_call" | custom-call | flops 33554432 | bytes 1048576 | tf_op jit(solution)/shard_map/sent_half/pallas_call | solution.py:144
  175.2 2.7 %collective-permute-start.3 = (f32[4,4,2,8,128]{4,3,2,1,0:T(8,128)S(1)}, f32[4,4,2,8,128]{4,3,2,1,0:T(8,128)S(1)}, u32[]{:S(2)}, u32[]{:S(2)}) collective-permute-start(f32[4,4,2,8,128]{4,3,2,1,0:T(8,128)S(1)} %get-tuple-element.37), channel_id=1, source_target_pairs={{0,2},{2,0},{4,6},{6,4},{8,10},{10,8},{12,14},{14,12},{16,18},{18,... | collective-permute-start | bytes 393224 | tf_op jit(solution)/shard_map/ppermute | solution.py:177
  178.0 4.8 %kept_half.7 = f32[4,4,2,8,128]{4,3,2,1,0:T(8,128)S(1)} custom-call(f32[8,512,128]{2,1,0:T(8,128)S(1)} %get-tuple-element.34.wide, f32[2,4,4,8,128]{4,3,2,1,0:T(8,128)S(1)} %get-tuple-element.35.turned, f32[32,4,8,128]{3,2,1,0:T(8,128)S(1)} %get-tuple-element.36.first), custom_call_target="tpu_custom_call" | custom-call | flops 33554432 | bytes 1048576 | tf_op jit(solution)/shard_map/kept_half/pallas_call | solution.py:144
  183.1 16.1 %all_to_all.69 = f32[32,2,8,128]{3,2,1,0:T(8,128)S(1)} all-to-all(f32[32,2,8,128]{3,2,1,0:T(8,128)S(1)} %pad_maximum_fusion), channel_id=1, replica_groups=mesh['x'=4,'y'=4,'z'=16,'k'=2] {'x','y','k'}, dimensions={0} | all-to-all | bytes 524288 | tf_op jit(solution)/shard_map/all_to_all | solution.py:157
  199.3 15.0 %all_to_all.70 = f32[16,2,8,128]{3,2,1,0:T(8,128)S(1)} all-to-all(f32[16,2,8,128]{3,2,1,0:T(8,128)S(1)} %pad_maximum_fusion.1), channel_id=1, replica_groups=mesh['x'=4,'y'=4,'z'=16,'k'=2] {'z'}, dimensions={0} | all-to-all | bytes 262144 | tf_op jit(solution)/shard_map/all_to_all | solution.py:157
  214.9 9.4 %all_to_all.71 = f32[16,2,8,128]{3,2,1,0:T(8,128)S(1)} all-to-all(f32[16,2,8,128]{3,2,1,0:T(8,128)S(1)} %broadcast_in_dim.31), channel_id=1, replica_groups=mesh['x'=4,'y'=4,'z'=16,'k'=2] {'x','y'}, dimensions={0} | all-to-all | bytes 262144 | tf_op jit(solution)/shard_map/all_to_all | solution.py:157
  (36 shorter events, 3.0 us)
Async XLA Ops:
  0.6 1.4 copy-start.1
  0.6 1.4 copy-start.2
  7.2 9.2 %collective-permute-start = (f32[4,4,2,8,128]{4,3,2,1,0:T(8,128)S(1)}, f32[4,4,2,8,128]{4,3,2,1,0:T(8,128)S(1)}, u32[]{:S(2)}, u32[]{:S(2)}) collective-permute-start(f32[4,4,2,8,128]{4,3,2,1,0:T(8,128)S(1)} %get-tuple-element.25), channel_id=1, source_target_pairs={{0,2},{2,0},{4,6},{6,4},{8,10},{10,8},{12,14},{14,12},{16,18},{18,... | collective-permute-start | bytes 393224 | tf_op jit(solution)/shard_map/ppermute | solution.py:177
  11.6 55.3 %copy-start = (bf16[4,512,1024]{2,1,0:T(8,128)(2,1)S(1)}, bf16[4,512,1024]{2,1,0:T(8,128)(2,1)}, u32[]{:S(2)}) copy-start(bf16[4,512,1024]{2,1,0:T(8,128)(2,1)} %delay_ref.5) | copy-start | bytes 12582916
  72.1 7.6 %collective-permute-start.1 = (f32[4,4,2,8,128]{4,3,2,1,0:T(8,128)S(1)}, f32[4,4,2,8,128]{4,3,2,1,0:T(8,128)S(1)}, u32[]{:S(2)}, u32[]{:S(2)}) collective-permute-start(f32[4,4,2,8,128]{4,3,2,1,0:T(8,128)S(1)} %get-tuple-element.29), channel_id=1, source_target_pairs={{0,2},{2,0},{4,6},{6,4},{8,10},{10,8},{12,14},{14,12},{16,18},{18,... | collective-permute-start | bytes 393224 | tf_op jit(solution)/shard_map/ppermute | solution.py:177
  123.7 7.6 %collective-permute-start.2 = (f32[4,4,2,8,128]{4,3,2,1,0:T(8,128)S(1)}, f32[4,4,2,8,128]{4,3,2,1,0:T(8,128)S(1)}, u32[]{:S(2)}, u32[]{:S(2)}) collective-permute-start(f32[4,4,2,8,128]{4,3,2,1,0:T(8,128)S(1)} %get-tuple-element.33), channel_id=1, source_target_pairs={{0,2},{2,0},{4,6},{6,4},{8,10},{10,8},{12,14},{14,12},{16,18},{18,... | collective-permute-start | bytes 393224 | tf_op jit(solution)/shard_map/ppermute | solution.py:177
  175.2 7.6 %collective-permute-start.3 = (f32[4,4,2,8,128]{4,3,2,1,0:T(8,128)S(1)}, f32[4,4,2,8,128]{4,3,2,1,0:T(8,128)S(1)}, u32[]{:S(2)}, u32[]{:S(2)}) collective-permute-start(f32[4,4,2,8,128]{4,3,2,1,0:T(8,128)S(1)} %get-tuple-element.37), channel_id=1, source_target_pairs={{0,2},{2,0},{4,6},{6,4},{8,10},{10,8},{12,14},{14,12},{16,18},{18,... | collective-permute-start | bytes 393224 | tf_op jit(solution)/shard_map/ppermute | solution.py:177
